TPU v7x, 8 devices: a whole 2x2x1 slice. The times are simulated.
8 devices in a mesh: terms: 8 (over z, y, x, core).
Axes of the slice: x: 2, y: 2, z: 1, core: 2. Of those that a mesh axis runs over, the one named last changes fastest.
Arguments:
- psi_init: float32 [896, 4, 4, 896], replicated
- left_env: bfloat16 [16, 896, 896], P('terms')
- op_pair: bfloat16 [16, 16, 16], P('terms')
- right_env: bfloat16 [16, 896, 896], P('terms')
Outputs:
- output 1: float32 [7, 896, 4, 4, 896], P(None, 'terms')
- output 2: float32 [6], replicated
- output 3: float32 [6], replicated
All inputs are finite; a program needn't handle non-finite values.
Results may differ from a plain program's by a relative error of at most 0.0161663.
Values are sent between devices in bfloat16 or wider.
A program may use at most 1 GiB of HBM per device.

v0:
```python
import jax
import jax.numpy as jnp
from jax import lax
from jax.sharding import PartitionSpec as P

KRYLOV_STEPS = 6


def solution(mesh):
    group_size = mesh.shape['terms']

    def local_run(psi_init, left_env, op_pair, right_env):
        bond_dim = psi_init.shape[0]
        phys_dim = psi_init.shape[1]
        pair_dim = phys_dim * phys_dim
        elem_count = bond_dim * pair_dim * bond_dim
        slab_rows = bond_dim // group_size
        row_start = lax.axis_index('terms') * slab_rows
        psi_full = psi_init.reshape(bond_dim, pair_dim, bond_dim)
        full_norm = jnp.sqrt(jnp.sum(psi_full * psi_full) / elem_count)
        vector = lax.dynamic_slice_in_dim(psi_full, row_start, slab_rows, 0) / full_norm
        vectors = [vector]
        alphas = []
        betas = []
        prev_vector = vector
        for step_idx in range(KRYLOV_STEPS):
            whole_vector = lax.all_gather(vector.astype(jnp.bfloat16), 'terms', axis=0, tiled=True)
            y_part = jnp.einsum('apc,kbc->kapb', whole_vector, right_env, preferred_element_type=jnp.float32).astype(jnp.bfloat16)
            z_part = jnp.einsum('kqp,kapb->kaqb', op_pair, y_part, preferred_element_type=jnp.float32).astype(jnp.bfloat16)
            partial_sigma = jnp.einsum('kax,kxqb->aqb', left_env, z_part, preferred_element_type=jnp.float32)
            sigma_slab = lax.psum_scatter(partial_sigma, 'terms', scatter_dimension=0, tiled=True)
            alpha_val = lax.psum(jnp.sum(sigma_slab * vector), 'terms') / elem_count
            residual = sigma_slab - alpha_val * vector
            if step_idx > 0:
                residual = residual - betas[-1] * prev_vector
            beta_val = jnp.sqrt(lax.psum(jnp.sum(residual * residual), 'terms') / elem_count)
            prev_vector = vector
            vector = residual / beta_val
            vectors.append(vector)
            alphas.append(alpha_val)
            betas.append(beta_val)
        krylov_vectors = jnp.stack(vectors).reshape(KRYLOV_STEPS + 1, slab_rows, phys_dim, phys_dim, bond_dim)
        return krylov_vectors, jnp.stack(alphas), jnp.stack(betas)

    return jax.shard_map(local_run, mesh=mesh, in_specs=(P(), P('terms'), P('terms'), P('terms')), out_specs=(P(None, 'terms'), P(), P()), check_vma=False)
```

profile of v0, /device:TPU:0, one launch (start us, length us, event | category | flops | bytes accessed | tf_op | source)
XLA Modules:
  0.0 5146.8 jit_solution(2494692035871966429)
XLA Ops:
  103.8 124.3 %all-gather.7.cloned.1.call-done = bf16[896,16,896]{2,1,0:T(8,128)(2,1)} async-done(((bf16[112,16,896]{2,1,0:T(8,128)(2,1)}), bf16[896,16,896]{2,1,0:T(8,128)(2,1)}) %all-gather.7.cloned.1.call-update) | async-done | bytes 25690128 | tf_op jit(solution)/shard_map/all_gather | solution.py:27
  289.2 70.9 %copy.81 = bf16[896,16,2,896]{3,2,1,0:T(2,128)(2,1)} copy(bf16[896,16,2,896]{3,1,2,0:T(8,128)(2,1)} %convolution_convert_fusion.5) | data formatting | bytes 102760448
  402.3 74.6 %copy.25 = bf16[2,896,896,16]{1,2,0,3:T(8,128)(2,1)} copy(bf16[2,896,896,16]{2,3,1,0:T(8,128)(2,1)} %fusion.22) | data formatting | bytes 102760448 | tf_op jit(solution)/shard_map/kqp,kapb->kaqb/dot_general | solution.py:29
  589.0 278.8 %reduce-scatter.7.cloned.1.call-done = f32[112,16,896]{2,1,0:T(8,128)} async-done(((f32[896,16,896]{2,1,0:T(8,128)}), f32[112,16,896]{2,1,0:T(8,128)}) %reduce-scatter.7.cloned.1.call-update) | async-done | bytes 6422544 | tf_op jit(solution)/shard_map/reduce_scatter | solution.py:31
  939.2 123.0 %all-gather.9.cloned.1.call-done = bf16[896,16,896]{2,1,0:T(8,128)(2,1)} async-done(((bf16[112,16,896]{2,1,0:T(8,128)(2,1)}), bf16[896,16,896]{2,1,0:T(8,128)(2,1)}) %all-gather.9.cloned.1.call-update) | async-done | bytes 25690128 | tf_op jit(solution)/shard_map/all_gather | solution.py:27
  1123.3 70.9 %copy.80 = bf16[896,16,2,896]{3,2,1,0:T(2,128)(2,1)} copy(bf16[896,16,2,896]{3,1,2,0:T(8,128)(2,1)} %convolution_convert_fusion.4) | data formatting | bytes 102760448
  1236.4 74.6 %copy.30 = bf16[2,896,896,16]{1,2,0,3:T(8,128)(2,1)} copy(bf16[2,896,896,16]{2,3,1,0:T(8,128)(2,1)} %fusion.20) | data formatting | bytes 102760448 | tf_op jit(solution)/shard_map/kqp,kapb->kaqb/dot_general | solution.py:29
  1423.1 278.9 %reduce-scatter.9.cloned.1.call-done = f32[112,16,896]{2,1,0:T(8,128)} async-done(((f32[896,16,896]{2,1,0:T(8,128)}), f32[112,16,896]{2,1,0:T(8,128)}) %reduce-scatter.9.cloned.1.call-update) | async-done | bytes 6422544 | tf_op jit(solution)/shard_map/reduce_scatter | solution.py:31
  1775.6 123.0 %all-gather.11.cloned.1.call-done = bf16[896,16,896]{2,1,0:T(8,128)(2,1)} async-done(((bf16[112,16,896]{2,1,0:T(8,128)(2,1)}), bf16[896,16,896]{2,1,0:T(8,128)(2,1)}) %all-gather.11.cloned.1.call-update) | async-done | bytes 25690128 | tf_op jit(solution)/shard_map/all_gather | solution.py:27
  1959.7 70.9 %copy.79 = bf16[896,16,2,896]{3,2,1,0:T(2,128)(2,1)} copy(bf16[896,16,2,896]{3,1,2,0:T(8,128)(2,1)} %convolution_convert_fusion.3) | data formatting | bytes 102760448
  2072.8 74.6 %copy.35 = bf16[2,896,896,16]{1,2,0,3:T(8,128)(2,1)} copy(bf16[2,896,896,16]{2,3,1,0:T(8,128)(2,1)} %fusion.18) | data formatting | bytes 102760448 | tf_op jit(solution)/shard_map/kqp,kapb->kaqb/dot_general | solution.py:29
  2259.4 278.9 %reduce-scatter.11.cloned.1.call-done = f32[112,16,896]{2,1,0:T(8,128)} async-done(((f32[896,16,896]{2,1,0:T(8,128)}), f32[112,16,896]{2,1,0:T(8,128)}) %reduce-scatter.11.cloned.1.call-update) | async-done | bytes 6422544 | tf_op jit(solution)/shard_map/reduce_scatter | solution.py:31
  2612.1 123.0 %all-gather.13.cloned.1.call-done = bf16[896,16,896]{2,1,0:T(8,128)(2,1)} async-done(((bf16[112,16,896]{2,1,0:T(8,128)(2,1)}), bf16[896,16,896]{2,1,0:T(8,128)(2,1)}) %all-gather.13.cloned.1.call-update) | async-done | bytes 25690128 | tf_op jit(solution)/shard_map/all_gather | solution.py:27
  2796.1 70.9 %copy.78 = bf16[896,16,2,896]{3,2,1,0:T(2,128)(2,1)} copy(bf16[896,16,2,896]{3,1,2,0:T(8,128)(2,1)} %convolution_convert_fusion.2) | data formatting | bytes 102760448
  2909.2 74.6 %copy.40 = bf16[2,896,896,16]{1,2,0,3:T(8,128)(2,1)} copy(bf16[2,896,896,16]{2,3,1,0:T(8,128)(2,1)} %fusion.16) | data formatting | bytes 102760448 | tf_op jit(solution)/shard_map/kqp,kapb->kaqb/dot_general | solution.py:29
  3095.9 278.8 %reduce-scatter.13.cloned.1.call-done = f32[112,16,896]{2,1,0:T(8,128)} async-done(((f32[896,16,896]{2,1,0:T(8,128)}), f32[112,16,896]{2,1,0:T(8,128)}) %reduce-scatter.13.cloned.1.call-update) | async-done | bytes 6422544 | tf_op jit(solution)/shard_map/reduce_scatter | solution.py:31
  3448.4 123.0 %all-gather.15.cloned.1.call-done = bf16[896,16,896]{2,1,0:T(8,128)(2,1)} async-done(((bf16[112,16,896]{2,1,0:T(8,128)(2,1)}), bf16[896,16,896]{2,1,0:T(8,128)(2,1)}) %all-gather.15.cloned.1.call-update) | async-done | bytes 25690128 | tf_op jit(solution)/shard_map/all_gather | solution.py:27
  3632.4 70.9 %copy.77 = bf16[896,16,2,896]{3,2,1,0:T(2,128)(2,1)} copy(bf16[896,16,2,896]{3,1,2,0:T(8,128)(2,1)} %convolution_convert_fusion.1) | data formatting | bytes 102760448
  3745.5 74.6 %copy.45 = bf16[2,896,896,16]{1,2,0,3:T(8,128)(2,1)} copy(bf16[2,896,896,16]{2,3,1,0:T(8,128)(2,1)} %fusion.14) | data formatting | bytes 102760448 | tf_op jit(solution)/shard_map/kqp,kapb->kaqb/dot_general | solution.py:29
  3932.2 278.8 %reduce-scatter.15.cloned.1.call-done = f32[112,16,896]{2,1,0:T(8,128)} async-done(((f32[896,16,896]{2,1,0:T(8,128)}), f32[112,16,896]{2,1,0:T(8,128)}) %reduce-scatter.15.cloned.1.call-update) | async-done | bytes 6422544 | tf_op jit(solution)/shard_map/reduce_scatter | solution.py:31
  4284.7 123.0 %all-gather.17.cloned.1.call-done = bf16[896,16,896]{2,1,0:T(8,128)(2,1)} async-done(((bf16[112,16,896]{2,1,0:T(8,128)(2,1)}), bf16[896,16,896]{2,1,0:T(8,128)(2,1)}) %all-gather.17.cloned.1.call-update) | async-done | bytes 25690128 | tf_op jit(solution)/shard_map/all_gather | solution.py:27
  4468.7 70.9 %copy.76 = bf16[896,16,2,896]{3,2,1,0:T(2,128)(2,1)} copy(bf16[896,16,2,896]{3,1,2,0:T(8,128)(2,1)} %convolution_convert_fusion) | data formatting | bytes 102760448
  4581.8 74.6 %copy.50 = bf16[2,896,896,16]{1,2,0,3:T(8,128)(2,1)} copy(bf16[2,896,896,16]{2,3,1,0:T(8,128)(2,1)} %fusion.12) | data formatting | bytes 102760448 | tf_op jit(solution)/shard_map/kqp,kapb->kaqb/dot_general | solution.py:29
  4848.7 198.6 %reduce-scatter.17.cloned.1.call-done = f32[112,16,896]{2,1,0:T(8,128)} async-done(((f32[896,16,896]{2,1,0:T(8,128)}), f32[112,16,896]{2,1,0:T(8,128)}) %reduce-scatter.17.cloned.1.call-update) | async-done | bytes 6422544 | tf_op jit(solution)/shard_map/reduce_scatter | solution.py:31
  (113 shorter events, 1918.7 us)
Async XLA Ops:
  7.2 221.0 %copy-start = (bf16[2,896,896]{2,1,0:T(8,128)(2,1)S(1)}, bf16[2,896,896]{2,1,0:T(8,128)(2,1)}, u32[]{:S(2)}) copy-start(bf16[2,896,896]{2,1,0:T(8,128)(2,1)} %param.7) | copy-start | bytes 9633796
  7.2 220.9 %all-gather.7.cloned.1.call-start = ((), (), s32[]{:S(2)}) async-start(), calls=%async_computation.6 | async-start | bytes 28901376 | tf_op jit(solution)/shard_map/all_gather | solution.py:27
  103.3 764.5 %reduce-scatter.7.cloned.1.call-start = ((), (), s32[]{:S(2)}) async-start(), calls=%async_computation.7 | async-start | bytes 57802752 | tf_op jit(solution)/shard_map/reduce_scatter | solution.py:31
  289.2 70.9 %copy-start.2 = (bf16[2,16,16]{2,1,0:T(8,128)(2,1)S(1)}, bf16[2,16,16]{2,1,0:T(8,128)(2,1)}, u32[]{:S(2)}) copy-start(bf16[2,16,16]{2,1,0:T(8,128)(2,1)} %param.6) | copy-start | bytes 3076
  588.5 473.7 %all-gather.9.cloned.1.call-start = ((), (), s32[]{:S(2)}) async-start(), calls=%async_computation.8 | async-start | bytes 28901376 | tf_op jit(solution)/shard_map/all_gather | solution.py:27
  939.2 762.7 %reduce-scatter.9.cloned.1.call-start = ((), (), s32[]{:S(2)}) async-start(), calls=%async_computation.9 | async-start | bytes 57802752 | tf_op jit(solution)/shard_map/reduce_scatter | solution.py:31
  1123.3 70.9 %copy-start.3 = (bf16[2,16,16]{2,1,0:T(8,128)(2,1)S(1)}, bf16[2,16,16]{2,1,0:T(8,128)(2,1)}, u32[]{:S(2)}) copy-start(bf16[2,16,16]{2,1,0:T(8,128)(2,1)} %param.6) | copy-start | bytes 3076
  1422.6 476.0 %all-gather.11.cloned.1.call-start = ((), (), s32[]{:S(2)}) async-start(), calls=%async_computation.10 | async-start | bytes 28901376 | tf_op jit(solution)/shard_map/all_gather | solution.py:27
  1775.6 762.7 %reduce-scatter.11.cloned.1.call-start = ((), (), s32[]{:S(2)}) async-start(), calls=%async_computation.11 | async-start | bytes 57802752 | tf_op jit(solution)/shard_map/reduce_scatter | solution.py:31
  1959.7 70.9 %copy-start.4 = (bf16[2,16,16]{2,1,0:T(8,128)(2,1)S(1)}, bf16[2,16,16]{2,1,0:T(8,128)(2,1)}, u32[]{:S(2)}) copy-start(bf16[2,16,16]{2,1,0:T(8,128)(2,1)} %param.6) | copy-start | bytes 3076
  2259.0 476.1 %all-gather.13.cloned.1.call-start = ((), (), s32[]{:S(2)}) async-start(), calls=%async_computation.12 | async-start | bytes 28901376 | tf_op jit(solution)/shard_map/all_gather | solution.py:27
  2612.0 762.7 %reduce-scatter.13.cloned.1.call-start = ((), (), s32[]{:S(2)}) async-start(), calls=%async_computation.13 | async-start | bytes 57802752 | tf_op jit(solution)/shard_map/reduce_scatter | solution.py:31
  2796.1 70.9 %copy-start.5 = (bf16[2,16,16]{2,1,0:T(8,128)(2,1)S(1)}, bf16[2,16,16]{2,1,0:T(8,128)(2,1)}, u32[]{:S(2)}) copy-start(bf16[2,16,16]{2,1,0:T(8,128)(2,1)} %param.6) | copy-start | bytes 3076
  3095.4 475.9 %all-gather.15.cloned.1.call-start = ((), (), s32[]{:S(2)}) async-start(), calls=%async_computation.14 | async-start | bytes 28901376 | tf_op jit(solution)/shard_map/all_gather | solution.py:27
  3448.3 762.7 %reduce-scatter.15.cloned.1.call-start = ((), (), s32[]{:S(2)}) async-start(), calls=%async_computation.15 | async-start | bytes 57802752 | tf_op jit(solution)/shard_map/reduce_scatter | solution.py:31
  3632.4 70.9 %copy-start.6 = (bf16[2,16,16]{2,1,0:T(8,128)(2,1)S(1)}, bf16[2,16,16]{2,1,0:T(8,128)(2,1)}, u32[]{:S(2)}) copy-start(bf16[2,16,16]{2,1,0:T(8,128)(2,1)} %param.6) | copy-start | bytes 3076
  3931.8 475.9 %all-gather.17.cloned.1.call-start = ((), (), s32[]{:S(2)}) async-start(), calls=%async_computation.16 | async-start | bytes 28901376 | tf_op jit(solution)/shard_map/all_gather | solution.py:27
  4284.6 762.7 %reduce-scatter.17.cloned.1.call-start = ((), (), s32[]{:S(2)}) async-start(), calls=%async_computation.17 | async-start | bytes 57802752 | tf_op jit(solution)/shard_map/reduce_scatter | solution.py:31
  4468.7 70.9 %copy-start.7 = (bf16[2,16,16]{2,1,0:T(8,128)(2,1)S(1)}, bf16[2,16,16]{2,1,0:T(8,128)(2,1)}, u32[]{:S(2)}) copy-start(bf16[2,16,16]{2,1,0:T(8,128)(2,1)} %param.6) | copy-start | bytes 3076
  5047.4 7.1 copy-start.1
Sparse Core Ops, SparseCore 0:
  103.4 124.6 all-gather.6
  588.6 279.1 reduce-scatter.6
  939.3 122.8 all-gather.8
  1422.7 279.1 reduce-scatter.8
  1775.7 122.8 all-gather.10
  2259.1 279.1 reduce-scatter.10
  2612.2 122.8 all-gather.12
  3095.6 279.1 reduce-scatter.12
  3448.5 122.8 all-gather.14
  3931.9 279.1 reduce-scatter.14
  4284.8 122.8 all-gather.16
  4768.2 279.1 reduce-scatter.16
where the time goes:
time: 5170 us; the launch traced here: 5150 us
  waiting for transfers between devices  2330 us (45%)
  local copies, waits for them, and re-layouts  1330 us (26%)
  matrix products  990 us (19%)
  blocking collectives  281 us (5%)
  other arithmetic  186 us (4%)
    reduce_scatter x6, waiting for transfers between devices, local_run(): lax.psum_scatter(partial_sigma, 'terms', scatter_dimension=0, tiled=True)  1590 us
    all_gather x6, waiting for transfers between devices, local_run(): lax.all_gather(vector.astype(jnp.bfloat16), 'terms', axis=0, tiled=True)  739 us
    unnamed x28, local copies, waits for them, and re-layouts  463 us
    dot_general x6, local copies, waits for them, and re-layouts, local_run(): jnp.einsum('kqp,kapb->kaqb', op_pair, y_part, preferred_element_type=jnp....  447 us
    dot_general x6, matrix products, local_run(): jnp.einsum('kax,kxqb->aqb', left_env, z_part, preferred_element_type=jnp....  371 us
    dot_general x6, matrix products, local_run(): jnp.einsum('apc,kbc->kapb', whole_vector, right_env, preferred_element_ty...  366 us
    dot_general x6, local copies, waits for them, and re-layouts, local_run(): jnp.einsum('kax,kxqb->aqb', left_env, z_part, preferred_element_type=jnp....  299 us
    dot_general x6, matrix products, local_run(): jnp.einsum('kqp,kapb->kaqb', op_pair, y_part, preferred_element_type=jnp....  253 us
  transfers between devices with their start and end apart: 12, of which 12 were waited for; matrix products, arithmetic and copies ran while one was open for 2% of the time, Pallas kernels for 0%

commit v1 on v0

v1 whole, which is shorter than its diff:
```python
import jax
import jax.numpy as jnp
from jax import lax
from jax.experimental import pallas as pl
from jax.experimental.pallas import tpu as pltpu
from jax.sharding import PartitionSpec as P

STEPS = 6
BOND = 896
NP = 16
TERMS = 16
NDEV = 8
ROWS = BOND // NDEV
LANES = 128
NCH = BOND // LANES
KG = 4
NKG = TERMS // KG
UNITS = NCH * NKG
SLAB = NP * ROWS
ELEMS = BOND * NP * BOND
MESH = pl.DeviceIdType.MESH
NS = ((0, 512), (512, 1024), (1024, 1536), (1536, 1792))


def kernel(v0_h, slab_h, left_h, kron_h, right_h, vout_h, ab_ref,
           vbuf, left, kron, rblk, sig, ubuf, zbuf, vecs, mine, exch,
           load_sem, v0_sem, r_sem, out_sem, send_sem, recv_sem, xs_sem, xr_sem):
    me = lax.axis_index('terms')
    core = lax.rem(me, 2)
    xpos = lax.rem(lax.div(me, 2), 2)
    ypos = lax.div(me, 4)
    sib = me + 1 - 2 * core
    xn = me + 2 - 4 * xpos
    yn = me + 4 - 8 * ypos
    dg = yn + 2 - 4 * xpos
    sx = xn + 1 - 2 * core
    sy = yn + 1 - 2 * core
    sd = dg + 1 - 2 * core

    def rows(dev):
        return pl.ds(pl.multiple_of(dev * ROWS, 16), ROWS)

    LO, HI, ALL = pl.ds(0, NP // 2), pl.ds(NP // 2, NP // 2), pl.ds(0, NP)
    kinds = ((LO, me, xn, xn), (HI, me, xn, xn), (HI, me, yn, yn), (LO, me, yn, yn), (ALL, me, sib, sib),
             (LO, xn, yn, dg), (HI, yn, xn, dg), (ALL, xn, sib, sx), (ALL, yn, sib, sy), (ALL, dg, sib, sd))

    def send(c, kind):
        ps, origin, target, _ = kinds[kind]
        part = vbuf.at[c, ps, rows(origin), :]
        return pltpu.make_async_remote_copy(part, part, send_sem.at[c, kind], recv_sem.at[c, kind],
                                            device_id=(target,), device_id_type=MESH)

    def landed(c, kind):
        ps, _, target, origin = kinds[kind]
        part = vbuf.at[c, ps, rows(origin), :]
        pltpu.make_async_remote_copy(part, part, send_sem.at[c, kind], recv_sem.at[c, kind],
                                     device_id=(target,), device_id_type=MESH).wait_recv()

    def send_own(c):
        for kind in (0, 2, 1, 3, 4):
            send(c, kind).start()

    def relay_half(c):
        landed(c, 0)
        send(c, 5).start()
        landed(c, 2)
        send(c, 6).start()

    def relay_sib(c):
        landed(c, 1)
        send(c, 7).start()
        landed(c, 3)
        send(c, 8).start()

    def relay_diag(c):
        landed(c, 5)
        landed(c, 6)
        send(c, 9).start()

    def arrived(c):
        for kind in (4, 7, 8, 9):
            landed(c, kind)

    def local_chunk(c):
        return pltpu.make_async_copy(v0_h.at[c], vbuf.at[c], v0_sem.at[c])

    barrier = pltpu.get_barrier_semaphore()
    for off in range(1, NDEV):
        pl.semaphore_signal(barrier, inc=1, device_id=(lax.rem(me + off, NDEV),), device_id_type=MESH)
    pl.semaphore_wait(barrier, NDEV - 1)

    local_chunk(0).start()
    loads = [pltpu.make_async_copy(left_h, left, load_sem.at[0]),
             pltpu.make_async_copy(kron_h, kron, load_sem.at[1]),
             pltpu.make_async_copy(slab_h, vecs.at[0], load_sem.at[2])]
    for cp in loads:
        cp.start()
    for c in range(1, NCH):
        local_chunk(c).start()
    vecs[1] = jnp.zeros((SLAB, BOND), jnp.float32)
    for cp in loads:
        cp.wait()

    def fetch(u):
        kg, c, slot = lax.rem(u, NKG), lax.div(u, NKG), lax.rem(u, 2)
        return [pltpu.make_async_copy(
            right_h.at[kg * KG + k, :, pl.ds(pl.multiple_of(c * LANES, LANES), LANES)],
            rblk.at[slot, :, pl.ds(k * LANES, LANES)], r_sem.at[slot, k]) for k in range(KG)]

    def stage_left(u):
        kg, c = lax.rem(u, NKG), lax.div(u, NKG)
        lhs = left[pl.ds(pl.multiple_of(kg * KG * ROWS, 64), KG * ROWS), :]
        for g in range(NP // 4):
            rhs = jnp.concatenate([vbuf[c, 4 * g + i] for i in range(4)], axis=1)
            o = jnp.dot(lhs, rhs, preferred_element_type=jnp.float32).astype(jnp.bfloat16)
            for i in range(4):
                ubuf[4 * g + i] = o[:, i * LANES:(i + 1) * LANES]

    def stage_pair(u):
        kg = lax.rem(u, NKG)
        for k in range(KG):
            rhs = jnp.concatenate([ubuf[:, k * ROWS + g * 16:k * ROWS + (g + 1) * 16, :].reshape(256, LANES)
                                   for g in range(ROWS // 16)], axis=1)
            o = jnp.dot(kron[kg * KG + k], rhs, preferred_element_type=jnp.float32).astype(jnp.bfloat16)
            for g in range(ROWS // 16):
                for q in range(NP):
                    zbuf[q * ROWS + g * 16:q * ROWS + (g + 1) * 16, k * LANES:(k + 1) * LANES] = (
                        o[q * 16:(q + 1) * 16, g * LANES:(g + 1) * LANES])

    def stage_right(u):
        slot = lax.rem(u, 2)
        for n0, n1 in NS:
            o = lax.dot_general(rblk[slot], zbuf[n0:n1, :], (((1,), (1,)), ((), ())),
                                preferred_element_type=jnp.float32)
            sig[:, n0:n1] += o

    def fold(x):
        return jnp.sum(x.reshape(-1, 8, LANES), axis=0)

    def one_step(j, beta_prev):
        cur, prv = lax.rem(j, 2), lax.rem(j + 1, 2)

        def gather_at(u):
            c, r = lax.div(u, NKG), lax.rem(u, NKG)

            @pl.when((j == 0) & (r == 0))
            def _():
                local_chunk(c).wait()

            @pl.when((j > 0) & (r == 0))
            def _():
                arrived(c)

            @pl.when((j > 0) & (r == 1) & (c < NCH - 1))
            def _():
                relay_half(c + 1)

            @pl.when((j > 0) & (r == 1) & (c < NCH - 2))
            def _():
                send_own(c + 2)

            @pl.when((j > 0) & (r == 2) & (c < NCH - 1))
            def _():
                relay_sib(c + 1)

            @pl.when((j > 0) & (r == 3) & (c < NCH - 1))
            def _():
                relay_diag(c + 1)

        for cp in fetch(0):
            cp.start()
        sig[...] = jnp.zeros((BOND, SLAB), jnp.float32)

        @pl.when(j > 0)
        def _():
            relay_half(0)
            send_own(1)
            relay_sib(0)
            relay_diag(0)

        gather_at(0)
        stage_left(0)
        gather_at(1)
        for cp in fetch(1):
            cp.start()
        stage_pair(0)
        stage_left(1)

        def unit(u, carry):
            gather_at(u)
            for cp in fetch(u - 2):
                cp.wait()
            stage_right(u - 2)
            stage_pair(u - 1)
            stage_left(u)
            for cp in fetch(u):
                cp.start()
            return carry

        lax.fori_loop(2, UNITS, unit, 0)
        for cp in fetch(UNITS - 2):
            cp.wait()
        stage_right(UNITS - 2)
        stage_pair(UNITS - 1)
        for cp in fetch(UNITS - 1):
            cp.wait()
        stage_right(UNITS - 1)

        def first(i, sums):
            a_sum, b_sum, v_sum = sums
            at = pl.ds(pl.multiple_of(i * LANES, LANES), LANES)
            for c in range(NCH):
                cs = slice(c * LANES, (c + 1) * LANES)
                tile = sig[cs, at].T
                v = vecs[cur, at, cs]
                s = tile - beta_prev * vecs[prv, at, cs]
                vecs[prv, at, cs] = s
                a_sum = a_sum + fold(tile * v)
                b_sum = b_sum + fold(s * v)
                v_sum = v_sum + fold(v * v)
            return a_sum, b_sum, v_sum

        zero = jnp.zeros((8, LANES), jnp.float32)
        a_sum, b_sum, v_sum = lax.fori_loop(0, SLAB // LANES, first, (zero, zero, zero), unroll=2)
        a_loc, b_loc, v_loc = jnp.sum(a_sum), jnp.sum(b_sum), jnp.sum(v_sum)
        a_row = jnp.full((8, LANES), a_loc)
        v_row = jnp.full((8, LANES), v_loc)
        fit = jnp.where(v_row > 0, jnp.full((8, LANES), b_loc) / jnp.where(v_row > 0, v_row, 1.0), 0.0)
        fit_row = fit[0:1, :]

        def second(i, n_sum):
            at = pl.ds(pl.multiple_of(i * LANES, LANES), LANES)
            for c in range(NCH):
                cs = slice(c * LANES, (c + 1) * LANES)
                d = vecs[prv, at, cs] - fit_row * vecs[cur, at, cs]
                n_sum = n_sum + fold(d * d)
            return n_sum

        n_loc = jnp.sum(lax.fori_loop(0, SLAB // LANES, second, zero, unroll=2))

        @pl.when(j > 0)
        def _():
            def sent(c, carry):
                for kind in range(len(kinds)):
                    send(c, kind).wait_send()
                return carry
            lax.fori_loop(0, NCH, sent, 0)

        @pl.when(j > 0)
        def _():
            pltpu.make_async_copy(vecs.at[cur], vout_h.at[j - 1], out_sem.at[0]).wait()

        row_id = lax.broadcasted_iota(jnp.int32, (8, LANES), 0)
        mine[...] = jnp.where(row_id == 0, a_row, jnp.where(
            row_id == 1, v_row, jnp.where(row_id == 2, fit, jnp.full((8, LANES), n_loc))))
        par = lax.rem(j, 2)
        exch[par, me] = mine[...]
        copies = []
        for off in range(1, NDEV):
            copies.append(pltpu.make_async_remote_copy(
                mine, exch.at[par, me], xs_sem.at[off - 1], xr_sem.at[par, off - 1],
                device_id=(lax.rem(me + off, NDEV),), device_id_type=MESH))
        for cp in copies:
            cp.start()
        for off in range(1, NDEV):
            src = lax.rem(me + NDEV - off, NDEV)
            pltpu.make_async_remote_copy(
                mine, exch.at[par, src], xs_sem.at[off - 1], xr_sem.at[par, off - 1],
                device_id=(src,), device_id_type=MESH).wait_recv()
        for cp in copies:
            cp.wait_send()
        total = exch[par, 0]
        for d in range(1, NDEV):
            total = total + exch[par, d]
        alpha = total[0:1, :] * (1.0 / ELEMS)
        square = jnp.zeros((1, LANES), jnp.float32)
        for d in range(NDEV):
            part = exch[par, d]
            gap = alpha - part[2:3, :]
            square = square + (part[3:4, :] + gap * gap * part[1:2, :])
        beta = jnp.sqrt(square * (1.0 / ELEMS))
        inv = 1.0 / beta
        ab_ref[j] = jnp.concatenate([alpha, beta] + [alpha] * 6, axis=0)

        for c in range(NCH):
            cs = slice(c * LANES, (c + 1) * LANES)

            def third(p, carry, c=c, cs=cs):
                at = pl.ds(pl.multiple_of(p * ROWS, 16), ROWS)
                n = (vecs[prv, at, cs] - alpha * vecs[cur, at, cs]) * inv
                vecs[prv, at, cs] = n
                vbuf[c, p, rows(me), :] = n.astype(jnp.bfloat16)
                return carry

            lax.fori_loop(0, NP, third, 0, unroll=4)
            if c == 1:
                @pl.when(j < STEPS - 1)
                def _():
                    send_own(0)
        pltpu.make_async_copy(vecs.at[prv], vout_h.at[j], out_sem.at[0]).start()
        return beta

    lax.fori_loop(0, STEPS, one_step, jnp.zeros((1, LANES), jnp.float32))
    pltpu.make_async_copy(vecs.at[STEPS % 2], vout_h.at[STEPS - 1], out_sem.at[0]).wait()


def lanczos(v0_low, v0_slab, left, kron, right):
    dma = pltpu.SemaphoreType.DMA
    return pl.pallas_call(
        kernel,
        out_shape=(jax.ShapeDtypeStruct((STEPS, SLAB, BOND), jnp.float32),
                   jax.ShapeDtypeStruct((STEPS, 8, LANES), jnp.float32)),
        in_specs=[pl.BlockSpec(memory_space=pl.ANY)] * 5,
        out_specs=(pl.BlockSpec(memory_space=pl.ANY), pl.BlockSpec(memory_space=pltpu.VMEM)),
        scratch_shapes=[
            pltpu.VMEM((NCH, NP, BOND, LANES), jnp.bfloat16),
            pltpu.VMEM((TERMS * ROWS, BOND), jnp.bfloat16),
            pltpu.VMEM((TERMS, 256, 256), jnp.bfloat16),
            pltpu.VMEM((2, BOND, KG * LANES), jnp.bfloat16),
            pltpu.VMEM((BOND, SLAB), jnp.float32),
            pltpu.VMEM((NP, KG * ROWS, LANES), jnp.bfloat16),
            pltpu.VMEM((SLAB, KG * LANES), jnp.bfloat16),
            pltpu.VMEM((2, SLAB, BOND), jnp.float32),
            pltpu.VMEM((8, LANES), jnp.float32),
            pltpu.VMEM((2, NDEV, 8, LANES), jnp.float32),
            dma((3,)), dma((NCH,)), dma((2, KG)), dma((1,)),
            dma((NCH, 10)), dma((NCH, 10)), dma((NDEV - 1,)), dma((2, NDEV - 1)),
        ],
        compiler_params=pltpu.CompilerParams(collective_id=0, has_side_effects=True, vmem_limit_bytes=67043328),
    )(v0_low, v0_slab, left, kron, right)


def solution(mesh):
    def local_run(psi_init, left_env, op_pair, right_env):
        row_start = lax.axis_index('terms') * ROWS
        right = lax.all_gather(right_env, 'terms', axis=0, tiled=True)
        left = lax.all_to_all(left_env, 'terms', split_axis=1, concat_axis=0, tiled=True).reshape(TERMS * ROWS, BOND)
        pair = lax.all_gather(op_pair, 'terms', axis=0, tiled=True)
        eye = jnp.eye(16, dtype=jnp.bfloat16)
        kron = (pair[:, :, None, :, None] * eye[None, None, :, None, :]).reshape(TERMS, 256, 256)
        psi = psi_init.reshape(BOND, NP, BOND)
        norm = jnp.sqrt(jnp.sum(psi * psi) / ELEMS)
        v0 = psi / norm
        v0_low = v0.astype(jnp.bfloat16).reshape(BOND, NP, NCH, LANES).transpose(2, 1, 0, 3)
        v0_own = lax.dynamic_slice_in_dim(psi, row_start, ROWS, 0) / norm
        v0_slab = v0_own.transpose(1, 0, 2).reshape(SLAB, BOND)
        vout, ab = lanczos(v0_low, v0_slab, left, kron, right)
        later = vout.reshape(STEPS, NP, ROWS, BOND).transpose(0, 2, 1, 3)
        vectors = jnp.concatenate([v0_own[None], later], axis=0).reshape(STEPS + 1, ROWS, 4, 4, BOND)
        return vectors, ab[:, 0, 0], ab[:, 1, 0]

    return jax.shard_map(local_run, mesh=mesh, in_specs=(P(), P('terms'), P('terms'), P('terms')),
                         out_specs=(P(None, 'terms'), P(), P()), check_vma=False)
```

time: 5170 us -> 1250 us (0.24)
  waiting for transfers between devices: 2330 us -> 0.69 us
  local copies, waits for them, and re-layouts: 1330 us -> 212 us
  matrix products: 990 us -> 0 us
  Pallas kernels: 0 us -> 916 us
  blocking collectives: 281 us -> 12.7 us
  other arithmetic: 186 us -> 89.4 us
    reduce_scatter x6 -> x0, waiting for transfers between devices: 1590 us -> none  [local_run(): lax.psum_scatter(partial_sigma, 'terms', scatter_dimension=0, tiled=True)]
    dot_general x18 -> x0, matrix products: 990 us -> none  [the longest x6 371 us: local_run(): jnp.einsum('kax,kxqb->aqb', left_env, z_part, preferred_element_type=jnp....]
    pallas_call x0 -> x1, Pallas kernels: none -> 916 us  [lanczos(): pl.pallas_call(kernel, out_shape=(jax.ShapeDtypeStruct((STEPS, SLAB, BOND...]
    dot_general x12 -> x0, local copies, waits for them, and re-layouts: 746 us -> none  [the longest x6 447 us: local_run(): jnp.einsum('kqp,kapb->kaqb', op_pair, y_part, preferred_element_type=jnp....]
    all_gather x6 -> x1, waiting for transfers between devices: 739 us -> 0.01 us  [local_run(): right = lax.all_gather(right_env, 'terms', axis=0, tiled=True)]
    unnamed x28 -> x8, local copies, waits for them, and re-layouts: 463 us -> 68.9 us
    psum x12 -> x0, blocking collectives: 281 us -> none  [the longest x6 146 us: local_run(): lax.psum(jnp.sum(residual * residual), 'terms') / elem_count]
    reduce_sum x13 -> x1, other arithmetic: 135 us -> 29.1 us  [local_run(): norm = jnp.sqrt(jnp.sum(psi * psi) / ELEMS)]
  transfers between devices with their start and end apart: 12 -> 2, of which waited for: 12 -> 0; matrix products, arithmetic and copies ran while one was open for 2% -> 19% of each run, Pallas kernels for 0% -> 0%
where the time goes in v1:
time: 1250 us
  Pallas kernels  916 us (73%)
  local copies, waits for them, and re-layouts  212 us (17%)
  other arithmetic  89.4 us (7%)
  between operations  14.8 us (1%)
  blocking collectives  12.7 us (1%)
    pallas_call x1, Pallas kernels, lanczos(): pl.pallas_call(kernel, out_shape=(jax.ShapeDtypeStruct((STEPS, SLAB, BOND...  916 us
    unnamed x8, local copies, waits for them, and re-layouts  68.9 us
    concatenate x2, local copies, waits for them, and re-layouts, local_run(): jnp.concatenate([v0_own[None], later], axis=0)  38.5 us
    convert_element_type x1, local copies, waits for them, and re-layouts, local_run(): v0.astype(jnp.bfloat16).reshape(BOND, NP, NCH, LANES).transpose(2, 1, 0, 3)  36.5 us
    reshape x1, local copies, waits for them, and re-layouts, local_run(): psi = psi_init.reshape(BOND, NP, BOND)  34.7 us
    concatenate x1, other arithmetic, local_run(): jnp.concatenate([v0_own[None], later], axis=0)  30.2 us
    mul x4, local copies, waits for them, and re-layouts, local_run(): pair[:, :, None, :, None] * eye[None, None, :, None, :]  30.2 us
    reduce_sum x1, other arithmetic, local_run(): norm = jnp.sqrt(jnp.sum(psi * psi) / ELEMS)  29.1 us
  transfers between devices with their start and end apart: 2, of which 0 were waited for; matrix products, arithmetic and copies ran while one was open for 19% of the time, Pallas kernels for 0%

profile of v1, /device:TPU:0, one launch (start us, length us, event | category | flops | bytes accessed | tf_op | source)
XLA Modules:
  0.0 1250.4 jit_solution(15088272621764047189)
XLA Ops:
  7.2 0.0 all-gather.2.cloned.1.call-start
  7.2 0.7 all-gather.2.cloned.1.call-update
  7.9 6.9 copy.21
  14.8 4.3 all-to-all-start
  19.1 59.3 %copy.19 = f32[896,4,4,896]{0,3,2,1:T(8,128)} copy(f32[896,4,4,896]{3,2,1,0:T(4,128)} %param.4) | data formatting | bytes 102760448 | tf_op args[0]
  78.3 29.1 %multiply_reduce_fusion = f32[]{:T(128)} fusion(f32[896,4,4,896]{3,2,1,0:T(4,128)} %param.4), kind=kLoop, calls=%fused_computation.1 | loop fusion | flops 25690112 | bytes 51380228 | tf_op jit(solution)/shard_map/reduce_sum | solution.py:342
  108.1 25.2 %divide_convert_fusion = bf16[896,4,4,896]{0,3,2,1:T(8,128)(2,1)} fusion(f32[896,4,4,896]{0,3,2,1:T(8,128)} %copy.19, f32[]{:T(128)S(6)} %sqrt.3), kind=kLoop, calls=%fused_computation | loop fusion | flops 25690112 | bytes 77070336 | tf_op jit(solution)/shard_map/convert_element_type | solution.py:344
  133.3 34.7 %copy.24 = f32[896,4,4,896]{3,0,2,1:T(8,128)} copy(f32[896,4,4,896]{3,2,1,0:T(4,128)} %param.4) | data formatting | bytes 102760448 | tf_op jit(solution)/shard_map/reshape | solution.py:341
  168.1 36.5 %copy.20 = bf16[896,16,7,128]{3,0,1,2:T(8,128)(2,1)} copy(bf16[896,16,7,128]{0,3,2,1:T(8,128)(2,1)} %bitcast.21) | data formatting | bytes 51380224 | tf_op jit(solution)/shard_map/convert_element_type | solution.py:344
  204.5 12.7 %all_gather.6 = bf16[16,16,16]{2,1,0:T(8,128)(2,1)S(1)} all-gather(bf16[2,16,16]{2,1,0:T(8,128)(2,1)S(1)} %copy-done.2), channel_id=1, replica_groups=mesh['terms'=8] {'terms'}, dimensions={0}, use_global_device_ids=true | all-gather | bytes 9216 | tf_op jit(solution)/shard_map/all_gather | solution.py:338
  217.2 6.2 mul.29
  223.4 20.5 %mul.30 = bf16[16,256,256]{2,1,0:T(8,128)(2,1)} reshape(bf16[16,16,16,16,16]{4,3,2,1,0:T(8,128)(2,1)} %mul.29) | data formatting | bytes 4194304 | tf_op jit(solution)/shard_map/mul | solution.py:340
  244.0 1.2 mul.31
  245.2 2.2 mul.32
  247.4 3.4 dynamic-slice_divide_fusion
  250.8 0.0 copy-start
  250.8 2.7 copy-done
  253.5 5.2 copy.25
  258.7 1.5 broadcast_multiply_fusion.kron_h
  260.2 2.0 copy.22
  262.3 916.3 %shard_map.67 = (f32[6,1792,896]{2,1,0:T(8,128)}, f32[6,8,128]{2,1,0:T(8,128)}) custom-call(bf16[7,16,896,128]{3,2,1,0:T(8,128)(2,1)} %bitcast.20, f32[1792,896]{1,0:T(8,128)} %bitcast.24, bf16[1792,896]{1,0:T(8,128)(2,1)} %bitcast.27, bf16[16,256,256]{2,1,0:T(8,128)(2,1)} %broadcast_multiply_fusion.kron_h, ...), custom_call_target="tpu_custom_call" | custom-call | tf_op jit(solution)/shard_map/pallas_call | solution.py:309
  1178.6 33.3 %copy.26 = f32[6,112,4,4,896]{4,3,2,1,0:T(4,128)} copy(f32[6,112,4,4,896]{4,1,3,2,0:T(8,128)} %bitcast.25) | data formatting | bytes 77070336 | tf_op jit(solution)/shard_map/concatenate | solution.py:349
  1211.9 1.5 slice_reduce_fusion
  1213.3 30.2 %pad_maximum_fusion = f32[7,112,4,4,896]{4,3,2,1,0:T(4,128)} fusion(f32[6,112,4,4,896]{4,3,2,1,0:T(4,128)} %copy.26, f32[1,112,4,4,896]{4,3,2,1,0:T(4,128)} %copy.25), kind=kLoop, calls=%fused_computation.2 | loop fusion | flops 11239424 | bytes 89915392 | tf_op jit(solution)/shard_map/concatenate | solution.py:349
  (7 shorter events, 0.0 us)
Async XLA Ops:
  7.2 255.1 %all-gather.2.cloned.1.call-start = ((), (), s32[]{:S(2)}) async-start(), calls=%async_computation.1 | async-start | bytes 28901376 | tf_op jit(solution)/shard_map/all_gather | solution.py:336
  14.8 245.5 %all-to-all-start = ((bf16[2,896,896]{2,0,1:T(2,128)(2,1)}), bf16[2,896,896]{2,0,1:T(2,128)(2,1)S(1)}, u32[]{:S(2)}, u32[]{:S(2)}) async-start(bf16[2,896,896]{2,0,1:T(2,128)(2,1)} %copy.21), calls=%async_computation | async-start | bytes 6422528 | tf_op jit(solution)/shard_map/all_to_all | solution.py:337
  168.1 36.5 %copy-start.2 = (bf16[2,16,16]{2,1,0:T(8,128)(2,1)S(1)}, bf16[2,16,16]{2,1,0:T(8,128)(2,1)}, u32[]{:S(2)}) copy-start(bf16[2,16,16]{2,1,0:T(8,128)(2,1)} %param.6) | copy-start | bytes 3076
  247.4 11.4 copy-start.1
  250.8 2.7 copy-start
Sparse Core Ops, SparseCore 0:
  9.8 157.6 all-gather.1

commit v2 on v0

v2 whole, which is shorter than its diff:
```python
import jax
import jax.numpy as jnp
from jax import lax
from jax.experimental import pallas as pl
from jax.experimental.pallas import tpu as pltpu
from jax.sharding import PartitionSpec as P

STEPS = 6
BOND = 896
NP = 16
TERMS = 16
NDEV = 8
ROWS = BOND // NDEV
LANES = 128
NCH = BOND // LANES
KG = 4
NKG = TERMS // KG
UNITS = NCH * NKG
SLAB = NP * ROWS
SLOTS = SLAB // LANES
ELEMS = BOND * NP * BOND
MESH = pl.DeviceIdType.MESH
NS = ((0, 4), (4, 8), (8, 12), (12, 14))


def kernel(psi_h, left_h, pair_h, right_h, kry_h, rall_h, ab_ref,
           vbuf, left, wall, kron, rblk, sig, ubuf, zbuf, vec, scale, mine, exch,
           slab_sem, psi_sem, own_sem, ls_sem, lr_sem, ws_sem, wr_sem,
           r_sem, out_sem, send_sem, recv_sem, xs_sem, xr_sem):
    me = lax.axis_index('terms')
    core = lax.rem(me, 2)
    xpos = lax.rem(lax.div(me, 2), 2)
    ypos = lax.div(me, 4)
    sib = me + 1 - 2 * core
    xn = me + 2 - 4 * xpos
    yn = me + 4 - 8 * ypos
    dg = yn + 2 - 4 * xpos
    sx = xn + 1 - 2 * core
    sy = yn + 1 - 2 * core
    sd = dg + 1 - 2 * core
    others = (sib, xn, sx, yn, sy, dg, sd)

    def rows(dev):
        return pl.ds(pl.multiple_of(dev * ROWS, 16), ROWS)

    def lanes(c):
        return pl.ds(pl.multiple_of(c * LANES, LANES), LANES)

    def remote(src, dst, ssem, rsem, target):
        return pltpu.make_async_remote_copy(src, dst, ssem, rsem, device_id=(target,), device_id_type=MESH)

    v_kinds = ((0, 4, me, xn, xn), (0, 4, me, yn, yn), (0, 4, me, sib, sib), (0, 2, xn, yn, dg), (2, 2, yn, xn, dg),
               (0, 4, xn, sib, sx), (0, 4, yn, sib, sy), (0, 4, dg, sib, sd))
    NV = len(v_kinds)

    def v_part(first, count, origin, q):
        return vbuf.at[lax.div(q, 4), pl.ds(4 * lax.rem(q, 4) + first, count), rows(origin), :]

    def v_send(q, kind):
        first, count, origin, target, _ = v_kinds[kind]
        part = v_part(first, count, origin, q)
        remote(part, part, send_sem.at[kind], recv_sem.at[q * NV + kind], target).start()

    def v_landed(q, kind):
        first, count, _, target, origin = v_kinds[kind]
        part = v_part(first, count, origin, q)
        remote(part, part, send_sem.at[kind], recv_sem.at[q * NV + kind], target).wait_recv()

    def v_sent(kind):
        first, count, origin, target, _ = v_kinds[kind]
        part = vbuf.at[:, pl.ds(0, 4 * count), rows(origin), :]
        remote(part, part, send_sem.at[kind], recv_sem.at[kind], target).wait_send()

    def send_own(q):
        for kind in (0, 1, 2):
            v_send(q, kind)

    def relay_xy(q):
        v_landed(q, 0)
        v_send(q, 3)
        v_send(q, 5)
        v_landed(q, 1)
        v_send(q, 4)
        v_send(q, 6)

    def relay_diag(q):
        v_landed(q, 3)
        v_landed(q, 4)
        v_send(q, 7)

    def arrived(q):
        for kind in (2, 5, 6, 7):
            v_landed(q, kind)

    LO, HI, ALL = (0, 1), (1, 1), (0, 2)
    r_kinds = ((LO, me, xn, xn), (HI, me, xn, xn), (HI, me, yn, yn), (LO, me, yn, yn), (ALL, me, sib, sib),
               (LO, xn, yn, dg), (HI, yn, xn, dg), (ALL, xn, sib, sx), (ALL, yn, sib, sy), (ALL, dg, sib, sd))
    NR = len(r_kinds)

    def r_part(half, origin, c):
        return rall_h.at[pl.ds(2 * origin + half[0], half[1]), :, lanes(c)]

    def r_send(c, kind):
        half, origin, target, _ = r_kinds[kind]
        dst = r_part(half, origin, c)
        src = right_h.at[pl.ds(half[0], half[1]), :, lanes(c)] if kind < 5 else dst
        remote(src, dst, send_sem.at[kind], recv_sem.at[c * NR + kind], target).start()

    def r_landed(c, kind):
        half, _, target, origin = r_kinds[kind]
        part = r_part(half, origin, c)
        remote(part, part, send_sem.at[kind], recv_sem.at[c * NR + kind], target).wait_recv()

    def r_sent(kind):
        half, origin, target, _ = r_kinds[kind]
        part = rall_h.at[pl.ds(2 * origin + half[0], half[1])]
        remote(part, part, send_sem.at[kind], recv_sem.at[kind], target).wait_send()

    def left_copy(n):
        return remote(left_h.at[:, rows(others[n]), :], left.at[pl.ds(2 * me, 2)], ls_sem.at[n], lr_sem.at[n], others[n])

    def left_landed(n):
        part = left.at[pl.ds(2 * others[n], 2)]
        remote(part, part, ls_sem.at[n], lr_sem.at[n], others[n]).wait_recv()

    def pair_copy(n):
        return remote(pair_h, wall.at[pl.ds(2 * me, 2)], ws_sem.at[n], wr_sem.at[n], others[n])

    def pair_landed(n):
        part = wall.at[pl.ds(2 * others[n], 2)]
        remote(part, part, ws_sem.at[n], wr_sem.at[n], others[n]).wait_recv()

    def psi_copy(n):
        c, p, slot = lax.div(n, NP), lax.rem(n, NP), lax.rem(n, SLOTS)
        return pltpu.make_async_copy(psi_h.at[:, lax.div(p, 4), lax.rem(p, 4), lanes(c)], sig.at[:, lanes(slot)],
                                     psi_sem.at[slot])

    def vector_out(j):
        return [pltpu.make_async_copy(vec.at[pl.ds(p * ROWS, ROWS), :], kry_h.at[j, :, p // 4, p % 4, :],
                                      out_sem.at[p]) for p in range(NP)]

    def fold(x):
        return jnp.sum(x.reshape(-1, 8, LANES), axis=0)

    def exchange_start(par):
        exch[par, me] = mine[...]
        copies = [remote(mine, exch.at[par, me], xs_sem.at[n], xr_sem.at[par, n], others[n]) for n in range(NDEV - 1)]
        for cp in copies:
            cp.start()
        return copies

    def exchange_wait(par, copies):
        for n in range(NDEV - 1):
            remote(mine, exch.at[par, others[n]], xs_sem.at[n], xr_sem.at[par, n], others[n]).wait_recv()
        for cp in copies:
            cp.wait_send()

    barrier = pltpu.get_barrier_semaphore()
    for n in range(NDEV - 1):
        pl.semaphore_signal(barrier, inc=1, device_id=(others[n],), device_id_type=MESH)
    slab = [pltpu.make_async_copy(psi_h.at[rows(me), p // 4, p % 4, :], vec.at[pl.ds(p * ROWS, ROWS), :],
                                  slab_sem.at[p]) for p in range(NP)]
    for cp in slab:
        cp.start()
    own = [pltpu.make_async_copy(pair_h, wall.at[pl.ds(2 * me, 2)], own_sem.at[0]),
           pltpu.make_async_copy(left_h.at[:, rows(me), :], left.at[pl.ds(2 * me, 2)], own_sem.at[1])]
    for cp in own:
        cp.start()
    for n in range(SLOTS):
        psi_copy(n).start()
    zero = jnp.zeros((8, LANES), jnp.float32)
    for cp in slab:
        cp.wait()

    def squares(i, acc):
        at = pl.ds(pl.multiple_of(i * LANES, LANES), LANES)
        for c in range(NCH):
            x = vec[at, c * LANES:(c + 1) * LANES]
            acc = acc + fold(x * x)
        return acc

    mine[...] = jnp.full((8, LANES), jnp.sum(lax.fori_loop(0, SLOTS, squares, zero, unroll=2)))
    with jax.named_scope('barrier'):
        pl.semaphore_wait(barrier, NDEV - 1)
    copies = exchange_start(1)
    for n in range(NDEV - 1):
        pair_copy(n).start()
    for n in range(NDEV - 1):
        left_copy(n).start()

    def r_own(c):
        for kind in (4, 0, 2, 1, 3):
            r_send(c, kind)

    r_own(0)
    with jax.named_scope('exch0'):
        exchange_wait(1, copies)
    total = exch[1, 0]
    for d in range(1, NDEV):
        total = total + exch[1, d]
    scale[...] = 1.0 / jnp.sqrt(total * (1.0 / ELEMS))

    def normalise(i, carry):
        at = pl.ds(pl.multiple_of(i * LANES, LANES), LANES)
        for c in range(NCH):
            cs = slice(c * LANES, (c + 1) * LANES)
            vec[at, cs] = vec[at, cs] * scale[0:1, :]
        return carry

    lax.fori_loop(0, SLOTS, normalise, 0, unroll=2)
    for cp in vector_out(0):
        cp.start()

    def piece(n, carry):
        psi_copy(n).wait()
        vbuf[lax.div(n, NP), lax.rem(n, NP)] = (sig[:, lanes(lax.rem(n, SLOTS))] * scale[0:1, :]).astype(jnp.bfloat16)

        @pl.when(n + SLOTS < NP * NCH)
        def _():
            psi_copy(n + SLOTS).start()
        return carry

    with jax.named_scope('convert'):
        lax.fori_loop(0, NP * NCH, piece, 0)

    for n in range(NDEV - 1):
        pair_landed(n)
    for cp in own:
        cp.wait()
    spread = (lax.div(lax.broadcasted_iota(jnp.int32, (256, 16), 0), 16)
              == lax.broadcasted_iota(jnp.int32, (256, 16), 1)).astype(jnp.float32).astype(jnp.bfloat16)
    same = (lax.rem(lax.broadcasted_iota(jnp.int32, (256, 256), 0), 16)
            == lax.rem(lax.broadcasted_iota(jnp.int32, (256, 256), 1), 16))

    def expand(k, carry):
        tall = jnp.dot(spread, wall[k], preferred_element_type=jnp.float32).astype(jnp.bfloat16)
        full = lax.dot_general(tall, spread, (((1,), (1,)), ((), ())), preferred_element_type=jnp.float32)
        kron[k] = jnp.where(same, full, 0.0).astype(jnp.bfloat16)
        return carry

    with jax.named_scope('kron'):
        lax.fori_loop(0, TERMS, expand, 0, unroll=4)
    sig[...] = jnp.zeros((BOND, SLAB), jnp.float32)
    with jax.named_scope('leftwait'):
        for n in range(NDEV - 1):
            left_landed(n)

    chip = lax.div(me, 2)

    def group(rel):
        return chip + lax.rem(rel, 2) * (1 - 2 * xpos) + lax.div(rel, 2) * (2 - 4 * ypos)

    def fetch_start(w):
        c, rel, slot = lax.div(w, NKG), lax.rem(w, NKG), lax.rem(w, 2)
        kg = group(rel)
        for k in range(KG):
            dst = rblk.at[slot, :, pl.ds(k * LANES, LANES)]
            here = (rel == 0) & (core == k // 2)

            @pl.when(here)
            def _():
                pltpu.make_async_copy(right_h.at[k % 2, :, lanes(c)], dst, r_sem.at[slot, k]).start()

            @pl.when(jnp.logical_not(here))
            def _():
                pltpu.make_async_copy(rall_h.at[kg * KG + k, :, lanes(c)], dst, r_sem.at[slot, k]).start()

    def fetch_wait(slot):
        for k in range(KG):
            pltpu.make_async_copy(rall_h.at[k, :, lanes(0)], rblk.at[slot, :, pl.ds(k * LANES, LANES)],
                                  r_sem.at[slot, k]).wait()

    def stage_left(c, g):
        rhs = jnp.concatenate([vbuf[c, 4 * g + i] for i in range(4)], axis=1)
        for kg in range(NKG):
            lhs = left[kg * KG:(kg + 1) * KG].reshape(KG * ROWS, BOND)
            o = jnp.dot(lhs, rhs, preferred_element_type=jnp.float32).astype(jnp.bfloat16)
            for i in range(4):
                ubuf[4 * g + i, kg * KG * ROWS:(kg + 1) * KG * ROWS, :] = o[:, i * LANES:(i + 1) * LANES]

    def stage_pair(k):
        rhs = jnp.concatenate([ubuf[:, k * ROWS + g * 16:k * ROWS + (g + 1) * 16, :].reshape(256, LANES)
                               for g in range(ROWS // 16)], axis=1)
        o = jnp.dot(kron[k], rhs, preferred_element_type=jnp.float32).astype(jnp.bfloat16)
        kg, at = k // KG, (k % KG) * LANES
        for g in range(ROWS // 16):
            for q in range(NP):
                zbuf[kg, q * ROWS + g * 16:q * ROWS + (g + 1) * 16, at:at + LANES] = (
                    o[q * 16:(q + 1) * 16, g * LANES:(g + 1) * LANES])

    def stage_right(rel, slot, part):
        n0, n1 = NS[part][0] * LANES, NS[part][1] * LANES
        o = lax.dot_general(rblk[slot], zbuf[group(rel), n0:n1, :], (((1,), (1,)), ((), ())),
                            preferred_element_type=jnp.float32)
        sig[:, n0:n1] += o

    def one_step(j, carry):
        beta_prev, cross = carry

        def r_before(q):
            c, g = lax.div(q, NKG), lax.rem(q, NKG)

            @pl.when((g == 3) & (c < NCH))
            def _():
                for kind in (0, 2, 1, 3):
                    r_landed(c, kind)
                for kind in (5, 6, 7, 8):
                    r_send(c, kind)

            @pl.when((g == 3) & (c < NCH - 1))
            def _():
                r_own(c + 1)

            @pl.when((g == 1) & (c > 0))
            def _():
                r_landed(c - 1, 5)
                r_landed(c - 1, 6)
                r_send(c - 1, 9)

        def before(q):
            @pl.when(j == 0)
            def _():
                r_before(q)

            @pl.when(j > 0)
            def _():
                @pl.when(q < UNITS - 1)
                def _():
                    relay_diag(q + 1)

                @pl.when(q < UNITS - 2)
                def _():
                    relay_xy(q + 2)

                @pl.when(q < UNITS - 4)
                def _():
                    send_own(q + 4)

                arrived(q)

        def first_chunk(g):
            @pl.when(j > 0)
            def _():
                relay_xy(g + 1)
                send_own(g + 3)
                relay_diag(g)
                arrived(g)

        def after(q):
            @pl.when(j == 0)
            def _():
                c, g = lax.div(q, NKG), lax.rem(q, NKG)
                for at, lag, kind in ((2, 0, 4), (3, 0, 7), (0, 1, 8), (1, 1, 9)):
                    @pl.when(g == at)
                    def _(lag=lag, kind=kind):
                        r_landed(c - lag, kind)

            fetch_start(q - 2)

        @pl.when(j > 0)
        def _():
            relay_xy(0)
            send_own(2)

        def opening(g, carry):
            with jax.named_scope('first'):
                first_chunk(g)
            with jax.named_scope('L'):
                stage_left(0, g)
            return carry

        lax.fori_loop(0, 2, opening, 0)
        first_chunk(2)
        with jax.named_scope('L'):
            stage_left(0, 2)
        with jax.named_scope('r1'):
            after(2)

            @pl.when(j == 0)
            def _():
                r_before(3)
            first_chunk(3)
        with jax.named_scope('LW'):
            stage_left(0, 3)
            for k in range(TERMS):
                stage_pair(k)
        with jax.named_scope('r2'):
            after(3)

            @pl.when(j > 0)
            def _():
                relay_diag(4)
                relay_xy(5)
                send_own(7)

        def chunk(c, carry):
            def unit(g, carry):
                q, slot = NKG * c + g, lax.rem(g, 2)
                with jax.named_scope('before'):
                    before(q)
                with jax.named_scope('RL'):
                    fetch_wait(slot)
                    for part in range(len(NS)):
                        stage_right(g, slot, part)
                    stage_left(c, g)
                with jax.named_scope('after'):
                    after(q)
                return carry

            lax.fori_loop(0, NKG - 1, unit, 0)
            q = NKG * c + NKG - 1
            with jax.named_scope('before'):
                before(q)
            with jax.named_scope('LRW'):
                fetch_wait(1)
                stage_left(c, NKG - 1)
                for part in range(len(NS)):
                    stage_right(NKG - 1, 1, part)
                for k in range(TERMS):
                    stage_pair(k)
            with jax.named_scope('after'):
                after(q)
            return carry

        lax.fori_loop(1, NCH, chunk, 0)

        def tail(g, carry):
            @pl.when(j == 0)
            def _():
                r_before(UNITS + g)
            with jax.named_scope('tail'):
                fetch_wait(lax.rem(g, 2))
                for part in range(len(NS)):
                    stage_right(g, lax.rem(g, 2), part)

            @pl.when(g < 2)
            def _():
                after(UNITS + g)
            return carry

        lax.fori_loop(0, NKG - 1, tail, 0)

        with jax.named_scope('sent'):
            @pl.when(j == 0)
            def _():
                for kind in range(NR):
                    r_sent(kind)
                for n in range(NDEV - 1):
                    left_copy(n).wait_send()
                    pair_copy(n).wait_send()

            @pl.when(j > 0)
            def _():
                for kind in range(NV):
                    v_sent(kind)

        with jax.named_scope('last'):
            fetch_wait(1)
            b_sum, v_sum = zero, zero
            for part in range(len(NS)):
                stage_right(NKG - 1, 1, part)
                for i in range(*NS[part]):
                    at = slice(i * LANES, (i + 1) * LANES)
                    for c in range(NCH):
                        cs = slice(c * LANES, (c + 1) * LANES)
                        s = sig[cs, at].T
                        v = vec[at, cs]
                        sig[cs, at] = s
                        b_sum = b_sum + fold(s * v)
                        v_sum = v_sum + fold(v * v)

        b_row = jnp.full((8, LANES), jnp.sum(b_sum))
        v_row = jnp.full((8, LANES), jnp.sum(v_sum))
        a_row = b_row + beta_prev * cross
        fit = jnp.where(v_row > 0, b_row / jnp.where(v_row > 0, v_row, 1.0), 0.0)
        fit_row = fit[0:1, :]

        def second(i, n_sum):
            at = pl.ds(pl.multiple_of(i * LANES, LANES), LANES)
            for c in range(NCH):
                cs = slice(c * LANES, (c + 1) * LANES)
                d = sig[cs, at] - fit_row * vec[at, cs]
                n_sum = n_sum + fold(d * d)
            return n_sum

        with jax.named_scope('pass2'):
            n_loc = jnp.sum(lax.fori_loop(0, SLOTS, second, zero, unroll=2))
        for cp in vector_out(j):
            cp.wait()

        row_id = lax.broadcasted_iota(jnp.int32, (8, LANES), 0)
        mine[...] = jnp.where(row_id == 0, a_row, jnp.where(
            row_id == 1, v_row, jnp.where(row_id == 2, fit, jnp.full((8, LANES), n_loc))))
        par = lax.rem(j, 2)
        with jax.named_scope('exch'):
            exchange_wait(par, exchange_start(par))
        total = exch[par, 0]
        for d in range(1, NDEV):
            total = total + exch[par, d]
        alpha = total[0:1, :] * (1.0 / ELEMS)
        square = jnp.zeros((1, LANES), jnp.float32)
        for d in range(NDEV):
            part = exch[par, d]
            gap = alpha - part[2:3, :]
            square = square + (part[3:4, :] + gap * gap * part[1:2, :])
        beta = jnp.sqrt(square * (1.0 / ELEMS))
        inv = 1.0 / beta
        ab_ref[j] = jnp.concatenate([alpha, beta] + [alpha] * 6, axis=0)

        def third(c, x_sum):
            cs = lanes(c)
            for i in range(SLOTS):
                at = slice(i * LANES, (i + 1) * LANES)
                v = vec[at, cs]
                n = (sig[cs, at] - alpha * v) * inv
                x_sum = x_sum + fold(v * n)
                vec[at, cs] = n
                low = n.astype(jnp.bfloat16)
                for t in range(8):
                    p, a = divmod(8 * i + t, ROWS // 16)
                    vbuf[c, p, pl.ds(pl.multiple_of(me * ROWS + 16 * a, 16), 16), :] = low[16 * t:16 * t + 16]
                sig[cs, at] = (v * -beta).T

            @pl.when((c == 1) & (j < STEPS - 1))
            def _():
                send_own(0)
                send_own(1)
            return x_sum

        with jax.named_scope('pass3'):
            x_sum = lax.fori_loop(0, NCH, third, zero)
        for cp in vector_out(j + 1):
            cp.start()
        return beta, jnp.full((8, LANES), jnp.sum(x_sum))

    lax.fori_loop(0, STEPS, one_step, (jnp.zeros((1, LANES), jnp.float32), zero))
    for cp in vector_out(STEPS):
        cp.wait()


def lanczos(psi, left, pair, right):
    dma = pltpu.SemaphoreType.DMA
    return pl.pallas_call(
        kernel,
        out_shape=(jax.ShapeDtypeStruct((STEPS + 1, ROWS, 4, 4, BOND), jnp.float32),
                   jax.ShapeDtypeStruct((TERMS, BOND, BOND), jnp.bfloat16),
                   jax.ShapeDtypeStruct((STEPS, 8, LANES), jnp.float32)),
        in_specs=[pl.BlockSpec(memory_space=pl.ANY)] * 4,
        out_specs=(pl.BlockSpec(memory_space=pl.ANY), pl.BlockSpec(memory_space=pl.ANY),
                   pl.BlockSpec(memory_space=pltpu.VMEM)),
        scratch_shapes=[
            pltpu.VMEM((NCH, NP, BOND, LANES), jnp.bfloat16),
            pltpu.VMEM((TERMS, ROWS, BOND), jnp.bfloat16),
            pltpu.VMEM((TERMS, 16, 16), jnp.bfloat16),
            pltpu.VMEM((TERMS, 256, 256), jnp.bfloat16),
            pltpu.VMEM((2, BOND, KG * LANES), jnp.bfloat16),
            pltpu.VMEM((BOND, SLAB), jnp.float32),
            pltpu.VMEM((NP, TERMS * ROWS, LANES), jnp.bfloat16),
            pltpu.VMEM((NKG, SLAB, KG * LANES), jnp.bfloat16),
            pltpu.VMEM((SLAB, BOND), jnp.float32),
            pltpu.VMEM((8, LANES), jnp.float32),
            pltpu.VMEM((8, LANES), jnp.float32),
            pltpu.VMEM((2, NDEV, 8, LANES), jnp.float32),
            dma((NP,)), dma((SLOTS,)), dma((2,)), dma((NDEV - 1,)), dma((NDEV - 1,)), dma((NDEV - 1,)), dma((NDEV - 1,)),
            dma((2, KG)), dma((NP,)), dma((10,)), dma((UNITS * 8,)), dma((NDEV - 1,)), dma((2, NDEV - 1)),
        ],
        compiler_params=pltpu.CompilerParams(collective_id=0, has_side_effects=True, vmem_limit_bytes=67043328),
    )(psi, left, pair, right)


def solution(mesh):
    def local_run(psi_init, left_env, op_pair, right_env):
        vectors, _, ab = lanczos(psi_init, left_env, op_pair, right_env)
        return vectors, ab[:, 0, 0], ab[:, 1, 0]

    return jax.shard_map(local_run, mesh=mesh, in_specs=(P(), P('terms'), P('terms'), P('terms')),
                         out_specs=(P(None, 'terms'), P(), P()), check_vma=False)
```

time: 5170 us -> 955 us (0.18)
  waiting for transfers between devices: 2330 us -> 0 us
  local copies, waits for them, and re-layouts: 1330 us -> 31.4 us
  matrix products: 990 us -> 0 us
  Pallas kernels: 0 us -> 922 us
  blocking collectives: 281 us -> 0 us
  other arithmetic: 186 us -> 0 us
    reduce_scatter x6 -> x0, waiting for transfers between devices: 1590 us -> none  [local_run(): lax.psum_scatter(partial_sigma, 'terms', scatter_dimension=0, tiled=True)]
    dot_general x18 -> x0, matrix products: 990 us -> none  [the longest x6 371 us: local_run(): jnp.einsum('kax,kxqb->aqb', left_env, z_part, preferred_element_type=jnp....]
    pallas_call x0 -> x1, Pallas kernels: none -> 922 us  [lanczos(): pl.pallas_call(kernel, out_shape=(jax.ShapeDtypeStruct((STEPS + 1, ROWS,...]
    dot_general x12 -> x0, local copies, waits for them, and re-layouts: 746 us -> none  [the longest x6 447 us: local_run(): jnp.einsum('kqp,kapb->kaqb', op_pair, y_part, preferred_element_type=jnp....]
    all_gather x6 -> x0, waiting for transfers between devices: 739 us -> none  [local_run(): lax.all_gather(vector.astype(jnp.bfloat16), 'terms', axis=0, tiled=True)]
    unnamed x28 -> x1, local copies, waits for them, and re-layouts: 463 us -> 30 us
    psum x12 -> x0, blocking collectives: 281 us -> none  [the longest x6 146 us: local_run(): lax.psum(jnp.sum(residual * residual), 'terms') / elem_count]
    reduce_sum x13 -> x0, other arithmetic: 135 us -> none  [the longest x6 64 us: local_run(): jnp.sum(residual * residual)]
  transfers between devices with their start and end apart: 12 -> 0, of which waited for: 12 -> 0; matrix products, arithmetic and copies ran while one was open for 2% -> 0% of each run, Pallas kernels for 0% -> 0%
where the time goes in v2:
time: 955 us; the launch traced here: 954 us
  Pallas kernels  922 us (97%)
  local copies, waits for them, and re-layouts  31.4 us (3%)
    pallas_call x1, Pallas kernels, lanczos(): pl.pallas_call(kernel, out_shape=(jax.ShapeDtypeStruct((STEPS + 1, ROWS,...  922 us
    unnamed x1, local copies, waits for them, and re-layouts  30 us

profile of v2, /device:TPU:0, one launch (start us, length us, event | category | flops | bytes accessed | tf_op | source)
XLA Modules:
  0.0 954.5 jit_solution(13485107076807218244)
XLA Ops:
  0.6 922.4 %shard_map.67 = (f32[7,112,4,4,896]{4,3,2,1,0:T(4,128)}, bf16[16,896,896]{2,1,0:T(8,128)(2,1)}, f32[6,8,128]{2,1,0:T(8,128)}) custom-call(f32[896,4,4,896]{3,2,1,0:T(4,128)} %psi_h.1, bf16[2,896,896]{2,1,0:T(8,128)(2,1)} %left_h.1, bf16[2,16,16]{2,1,0:T(8,128)(2,1)} %pair_h.1, bf16[2,896,896]{2,1,0:T(8,128)(2,1)} %right_h.1), custom_call_target="tpu_custom_call" | custom-call | tf_op jit(solution)/shard_map/pallas_call | solution.py:543
  923.0 1.5 slice_reduce_fusion
  924.5 30.0 %copy.8 = f32[7,112,4,4,896]{4,3,2,1,0:T(4,128)} copy(f32[7,112,4,4,896]{4,3,2,1,0:T(4,128)} %get-tuple-element.12) | data formatting | bytes 89915392

commit v3 on v2

--- a/solution.py
+++ b/solution.py
@@ -25,7 +25,7 @@
 
 def kernel(psi_h, left_h, pair_h, right_h, kry_h, rall_h, ab_ref,
            vbuf, left, wall, kron, rblk, sig, ubuf, zbuf, vec, scale, mine, exch,
-           slab_sem, psi_sem, own_sem, ls_sem, lr_sem, ws_sem, wr_sem,
+           slab_sem, psi_sem, own_sem, rest_sem, ls_sem, lr_sem, ws_sem, wr_sem,
            r_sem, out_sem, send_sem, recv_sem, xs_sem, xr_sem):
     me = lax.axis_index('terms')
     core = lax.rem(me, 2)
@@ -53,44 +53,47 @@
                (0, 4, xn, sib, sx), (0, 4, yn, sib, sy), (0, 4, dg, sib, sd))
     NV = len(v_kinds)
 
-    def v_part(first, count, origin, q):
-        return vbuf.at[lax.div(q, 4), pl.ds(4 * lax.rem(q, 4) + first, count), rows(origin), :]
-
-    def v_send(q, kind):
+    def v_part(first, count, origin, c, g):
+        return vbuf.at[c, pl.ds(4 * g + first, count), rows(origin), :]
+
+    def v_sem(c, g, kind):
+        return recv_sem.at[c * (NV * NKG) + g * NV + kind]
+
+    def v_send(c, g, kind):
         first, count, origin, target, _ = v_kinds[kind]
-        part = v_part(first, count, origin, q)
-        remote(part, part, send_sem.at[kind], recv_sem.at[q * NV + kind], target).start()
-
-    def v_landed(q, kind):
+        part = v_part(first, count, origin, c, g)
+        remote(part, part, send_sem.at[kind], v_sem(c, g, kind), target).start()
+
+    def v_landed(c, g, kind):
         first, count, _, target, origin = v_kinds[kind]
-        part = v_part(first, count, origin, q)
-        remote(part, part, send_sem.at[kind], recv_sem.at[q * NV + kind], target).wait_recv()
+        part = v_part(first, count, origin, c, g)
+        remote(part, part, send_sem.at[kind], v_sem(c, g, kind), target).wait_recv()
 
     def v_sent(kind):
         first, count, origin, target, _ = v_kinds[kind]
         part = vbuf.at[:, pl.ds(0, 4 * count), rows(origin), :]
         remote(part, part, send_sem.at[kind], recv_sem.at[kind], target).wait_send()
 
-    def send_own(q):
+    def send_own(c, g):
         for kind in (0, 1, 2):
-            v_send(q, kind)
-
-    def relay_xy(q):
-        v_landed(q, 0)
-        v_send(q, 3)
-        v_send(q, 5)
-        v_landed(q, 1)
-        v_send(q, 4)
-        v_send(q, 6)
-
-    def relay_diag(q):
-        v_landed(q, 3)
-        v_landed(q, 4)
-        v_send(q, 7)
-
-    def arrived(q):
+            v_send(c, g, kind)
+
+    def relay_xy(c, g):
+        v_landed(c, g, 0)
+        v_send(c, g, 3)
+        v_send(c, g, 5)
+        v_landed(c, g, 1)
+        v_send(c, g, 4)
+        v_send(c, g, 6)
+
+    def relay_diag(c, g):
+        v_landed(c, g, 3)
+        v_landed(c, g, 4)
+        v_send(c, g, 7)
+
+    def arrived(c, g):
         for kind in (2, 5, 6, 7):
-            v_landed(q, kind)
+            v_landed(c, g, kind)
 
     LO, HI, ALL = (0, 1), (1, 1), (0, 2)
     r_kinds = ((LO, me, xn, xn), (HI, me, xn, xn), (HI, me, yn, yn), (LO, me, yn, yn), (ALL, me, sib, sib),
@@ -166,6 +169,12 @@
            pltpu.make_async_copy(left_h.at[:, rows(me), :], left.at[pl.ds(2 * me, 2)], own_sem.at[1])]
     for cp in own:
         cp.start()
+    rest = [(h, c, rblk.at[(h * NCH + c) // KG, (h * NCH + c) % KG]) for h in range(2) for c in range(NCH)]
+    take = [pltpu.make_async_copy(right_h.at[h, :, lanes(c)], at, rest_sem.at[n]) for n, (h, c, at) in enumerate(rest)]
+    place_own = [pltpu.make_async_copy(at, rall_h.at[2 * me + h, :, lanes(c)], rest_sem.at[n])
+                 for n, (h, c, at) in enumerate(rest)]
+    for cp in take:
+        cp.start()
     for n in range(SLOTS):
         psi_copy(n).start()
     zero = jnp.zeros((8, LANES), jnp.float32)
@@ -185,14 +194,25 @@
     copies = exchange_start(1)
     for n in range(NDEV - 1):
         pair_copy(n).start()
-    for n in range(NDEV - 1):
+    for n in range(5):
         left_copy(n).start()
 
     def r_own(c):
         for kind in (4, 0, 2, 1, 3):
             r_send(c, kind)
 
-    r_own(0)
+    def operators_out(c, carry):
+        r_own(c)
+        return carry
+
+    lax.fori_loop(0, 5, operators_out, 0)
+    for n in (5, 6):
+        left_copy(n).start()
+    lax.fori_loop(5, NCH, operators_out, 0)
+    for cp in take:
+        cp.wait()
+    for cp in place_own:
+        cp.start()
     with jax.named_scope('exch0'):
         exchange_wait(1, copies)
     total = exch[1, 0]
@@ -210,18 +230,6 @@
     lax.fori_loop(0, SLOTS, normalise, 0, unroll=2)
     for cp in vector_out(0):
         cp.start()
-
-    def piece(n, carry):
-        psi_copy(n).wait()
-        vbuf[lax.div(n, NP), lax.rem(n, NP)] = (sig[:, lanes(lax.rem(n, SLOTS))] * scale[0:1, :]).astype(jnp.bfloat16)
-
-        @pl.when(n + SLOTS < NP * NCH)
-        def _():
-            psi_copy(n + SLOTS).start()
-        return carry
-
-    with jax.named_scope('convert'):
-        lax.fori_loop(0, NP * NCH, piece, 0)
 
     for n in range(NDEV - 1):
         pair_landed(n)
@@ -232,213 +240,235 @@
     same = (lax.rem(lax.broadcasted_iota(jnp.int32, (256, 256), 0), 16)
             == lax.rem(lax.broadcasted_iota(jnp.int32, (256, 256), 1), 16))
 
-    def expand(k, carry):
+    def piece(n):
+        vbuf[lax.div(n, NP), lax.rem(n, NP)] = (
+            sig[:, lanes(lax.rem(n, SLOTS))] * scale[0:1, :]).astype(jnp.bfloat16)
+
+    def opening_pieces(k, carry):
         tall = jnp.dot(spread, wall[k], preferred_element_type=jnp.float32).astype(jnp.bfloat16)
         full = lax.dot_general(tall, spread, (((1,), (1,)), ((), ())), preferred_element_type=jnp.float32)
         kron[k] = jnp.where(same, full, 0.0).astype(jnp.bfloat16)
+        for t in range(4):
+            n = 4 * k + t
+            psi_copy(n).wait()
+            piece(n)
+            psi_copy(n + SLOTS).start()
         return carry
 
-    with jax.named_scope('kron'):
-        lax.fori_loop(0, TERMS, expand, 0, unroll=4)
-    sig[...] = jnp.zeros((BOND, SLAB), jnp.float32)
-    with jax.named_scope('leftwait'):
-        for n in range(NDEV - 1):
-            left_landed(n)
+    with jax.named_scope('convert'):
+        lax.fori_loop(0, TERMS, opening_pieces, 0)
+    left_landed(0)
+    with jax.named_scope('ownwait'):
+        for cp in place_own:
+            cp.wait()
 
     chip = lax.div(me, 2)
 
     def group(rel):
         return chip + lax.rem(rel, 2) * (1 - 2 * xpos) + lax.div(rel, 2) * (2 - 4 * ypos)
 
-    def fetch_start(w):
-        c, rel, slot = lax.div(w, NKG), lax.rem(w, NKG), lax.rem(w, 2)
-        kg = group(rel)
-        for k in range(KG):
-            dst = rblk.at[slot, :, pl.ds(k * LANES, LANES)]
-            here = (rel == 0) & (core == k // 2)
-
-            @pl.when(here)
-            def _():
-                pltpu.make_async_copy(right_h.at[k % 2, :, lanes(c)], dst, r_sem.at[slot, k]).start()
-
-            @pl.when(jnp.logical_not(here))
-            def _():
-                pltpu.make_async_copy(rall_h.at[kg * KG + k, :, lanes(c)], dst, r_sem.at[slot, k]).start()
+    def place(j, u):
+        later = lax.div(j + STEPS - 1, STEPS)
+        t = lax.div(u, NCH)
+        mid, last = lax.div(t * (3 - t), 2), lax.div(t, 3)
+        rel0 = mid * (1 + lax.rem(u + 1, 2)) + last * 3
+        c0 = (1 - mid - last) * u + mid * lax.div(u - NCH, 2) + last * (u - 3 * NCH)
+        c = later * lax.div(u, NKG) + (1 - later) * c0
+        rel = later * lax.rem(u, NKG) + (1 - later) * rel0
+        return c, rel, group(rel)
+
+    def fetch_start(j, u, slot):
+        c, _, kg = place(j, u)
+        pltpu.make_async_copy(rall_h.at[pl.ds(kg * KG, KG), :, lanes(c)], rblk.at[slot], r_sem.at[slot]).start()
 
     def fetch_wait(slot):
-        for k in range(KG):
-            pltpu.make_async_copy(rall_h.at[k, :, lanes(0)], rblk.at[slot, :, pl.ds(k * LANES, LANES)],
-                                  r_sem.at[slot, k]).wait()
-
-    def stage_left(c, g):
-        rhs = jnp.concatenate([vbuf[c, 4 * g + i] for i in range(4)], axis=1)
-        for kg in range(NKG):
-            lhs = left[kg * KG:(kg + 1) * KG].reshape(KG * ROWS, BOND)
+        pltpu.make_async_copy(rall_h.at[pl.ds(0, KG), :, lanes(0)], rblk.at[slot], r_sem.at[slot]).wait()
+
+    def stage_left(j, s, g):
+        for i in range(NKG):
+            c, _, kg = place(j, NKG * s + i)
+            rhs = jnp.concatenate([vbuf[c, 4 * g + t] for t in range(4)], axis=1)
+            lhs = left[pl.ds(kg * KG, KG)].reshape(KG * ROWS, BOND)
             o = jnp.dot(lhs, rhs, preferred_element_type=jnp.float32).astype(jnp.bfloat16)
-            for i in range(4):
-                ubuf[4 * g + i, kg * KG * ROWS:(kg + 1) * KG * ROWS, :] = o[:, i * LANES:(i + 1) * LANES]
-
-    def stage_pair(k):
-        rhs = jnp.concatenate([ubuf[:, k * ROWS + g * 16:k * ROWS + (g + 1) * 16, :].reshape(256, LANES)
-                               for g in range(ROWS // 16)], axis=1)
-        o = jnp.dot(kron[k], rhs, preferred_element_type=jnp.float32).astype(jnp.bfloat16)
-        kg, at = k // KG, (k % KG) * LANES
-        for g in range(ROWS // 16):
-            for q in range(NP):
-                zbuf[kg, q * ROWS + g * 16:q * ROWS + (g + 1) * 16, at:at + LANES] = (
-                    o[q * 16:(q + 1) * 16, g * LANES:(g + 1) * LANES])
-
-    def stage_right(rel, slot, part):
+            for t in range(4):
+                ubuf[4 * g + t, i * KG * ROWS:(i + 1) * KG * ROWS, :] = o[:, t * LANES:(t + 1) * LANES]
+
+    def stage_pair(j, s):
+        for i in range(NKG):
+            _, _, kg = place(j, NKG * s + i)
+            for k in range(KG):
+                row, at = (i * KG + k) * ROWS, k * LANES
+                rhs = jnp.concatenate([ubuf[:, row + g * 16:row + (g + 1) * 16, :].reshape(256, LANES)
+                                       for g in range(ROWS // 16)], axis=1)
+                o = jnp.dot(kron[kg * KG + k], rhs, preferred_element_type=jnp.float32).astype(jnp.bfloat16)
+                for g in range(ROWS // 16):
+                    for q in range(NP):
+                        zbuf[i, q * ROWS + g * 16:q * ROWS + (g + 1) * 16, at:at + LANES] = (
+                            o[q * 16:(q + 1) * 16, g * LANES:(g + 1) * LANES])
+
+    def stage_right(blocks, part):
         n0, n1 = NS[part][0] * LANES, NS[part][1] * LANES
-        o = lax.dot_general(rblk[slot], zbuf[group(rel), n0:n1, :], (((1,), (1,)), ((), ())),
-                            preferred_element_type=jnp.float32)
-        sig[:, n0:n1] += o
+        lhs = jnp.concatenate([rblk[slot, k] for _, slot in blocks for k in range(KG)], axis=1)
+        rhs = jnp.concatenate([zbuf[i, n0:n1, :] for i, _ in blocks], axis=1)
+        sig[:, n0:n1] += lax.dot_general(lhs, rhs, (((1,), (1,)), ((), ())), preferred_element_type=jnp.float32)
 
     def one_step(j, carry):
         beta_prev, cross = carry
 
         def r_before(q):
-            c, g = lax.div(q, NKG), lax.rem(q, NKG)
-
-            @pl.when((g == 3) & (c < NCH))
+            for at, group in ((NKG, (1, 2)), (2 * NKG, (3, 4)), (5 * NKG, (5, 6))):
+                @pl.when(q == at)
+                def _(group=group):
+                    for n in group:
+                        left_landed(n)
+
+            @pl.when((q >= 8) & (q < 8 + 2 * NCH) & (lax.rem(q, 2) == 0))
             def _():
+                c = lax.div(q - 8, 2)
                 for kind in (0, 2, 1, 3):
                     r_landed(c, kind)
                 for kind in (5, 6, 7, 8):
                     r_send(c, kind)
 
-            @pl.when((g == 3) & (c < NCH - 1))
+            @pl.when(q >= 22)
             def _():
-                r_own(c + 1)
-
-            @pl.when((g == 1) & (c > 0))
-            def _():
-                r_landed(c - 1, 5)
-                r_landed(c - 1, 6)
-                r_send(c - 1, 9)
-
-        def before(q):
+                c = q - 22
+                r_landed(c, 5)
+                r_landed(c, 6)
+                r_send(c, 9)
+
+        def fetch(u, slot=None):
             @pl.when(j == 0)
             def _():
-                r_before(q)
-
-            @pl.when(j > 0)
-            def _():
-                @pl.when(q < UNITS - 1)
+                @pl.when(u < NCH)
                 def _():
-                    relay_diag(q + 1)
-
-                @pl.when(q < UNITS - 2)
+                    r_landed(u, 4)
+
+                for odd, kind in ((1, 7), (0, 8)):
+                    @pl.when((u >= NCH) & (u < 3 * NCH) & (lax.rem(u, 2) == odd))
+                    def _(kind=kind):
+                        r_landed(lax.div(u - NCH, 2), kind)
+
+                @pl.when(u >= 3 * NCH)
                 def _():
-                    relay_xy(q + 2)
-
-                @pl.when(q < UNITS - 4)
+                    r_landed(u - 3 * NCH, 9)
+
+            fetch_start(j, u, lax.rem(u, NKG) if slot is None else slot)
+
+        def opening(g, carry):
+            with jax.named_scope('first'):
+                near, own = g + 1, g + 3
+                relay_xy(lax.div(near, NKG), lax.rem(near, NKG))
+                send_own(lax.div(own, NKG), lax.rem(own, NKG))
+                relay_diag(0, g)
+                arrived(0, g)
+            with jax.named_scope('L'):
+                stage_left(j, 0, g)
+            return carry
+
+        def opening_zero(g, carry):
+            each = 12
+            for t in range(each):
+                psi_copy(4 * NP + each * g + t).wait()
+            for t in range(each):
+                piece(4 * NP + each * g + t)
+            for t in range(each):
+                n = 4 * NP + each * g + t + SLOTS
+
+                @pl.when(n < NP * NCH)
                 def _():
-                    send_own(q + 4)
-
-                arrived(q)
-
-        def first_chunk(g):
-            @pl.when(j > 0)
-            def _():
-                relay_xy(g + 1)
-                send_own(g + 3)
-                relay_diag(g)
-                arrived(g)
-
-        def after(q):
-            @pl.when(j == 0)
-            def _():
-                c, g = lax.div(q, NKG), lax.rem(q, NKG)
-                for at, lag, kind in ((2, 0, 4), (3, 0, 7), (0, 1, 8), (1, 1, 9)):
-                    @pl.when(g == at)
-                    def _(lag=lag, kind=kind):
-                        r_landed(c - lag, kind)
-
-            fetch_start(q - 2)
+                    psi_copy(n).start()
+            stage_left(j, 0, g)
+            return carry
+
+        @pl.when(j == 0)
+        def _():
+            with jax.named_scope('L0'):
+                lax.fori_loop(0, NKG, opening_zero, 0)
+                sig[...] = jnp.zeros((BOND, SLAB), jnp.float32)
 
         @pl.when(j > 0)
         def _():
-            relay_xy(0)
-            send_own(2)
-
-        def opening(g, carry):
-            with jax.named_scope('first'):
-                first_chunk(g)
-            with jax.named_scope('L'):
-                stage_left(0, g)
+            relay_xy(0, 0)
+            send_own(0, 2)
+            lax.fori_loop(0, NKG, opening, 0)
+            with jax.named_scope('first3'):
+                relay_xy(1, 1)
+                send_own(1, 3)
+                relay_diag(1, 0)
+        for u in range(3):
+            fetch(u)
+        with jax.named_scope('W'):
+            stage_pair(j, 0)
+
+        def chunk(s, carry):
+            def unit(g, carry):
+                with jax.named_scope('before'):
+                    @pl.when(j == 0)
+                    def _():
+                        r_before(NKG * s + g)
+
+                    @pl.when(j > 0)
+                    def _():
+                        relay_diag(s, g + 1)
+
+                        @pl.when(NKG * s + g < UNITS - 2)
+                        def _():
+                            ahead = g + 2
+                            relay_xy(s + lax.div(ahead, NKG), lax.rem(ahead, NKG))
+
+                        @pl.when(s < NCH - 1)
+                        def _():
+                            send_own(s + 1, g)
+
+                        arrived(s, g)
+                with jax.named_scope('RL'):
+                    fetch_wait(g)
+                    stage_left(j, s, g)
+                    for part in range(len(NS)):
+                        stage_right(((g, g),), part)
+                with jax.named_scope('after'):
+                    fetch(NKG * s + g - 1)
+                return carry
+
+            lax.fori_loop(0, NKG - 1, unit, 0)
+            with jax.named_scope('before'):
+                @pl.when(j == 0)
+                def _():
+                    r_before(NKG * s + NKG - 1)
+
+                @pl.when(j > 0)
+                def _():
+                    @pl.when(s < NCH - 1)
+                    def _():
+                        relay_diag(s + 1, 0)
+                        relay_xy(s + 1, 1)
+                        send_own(s + 1, 3)
+
+                    @pl.when(s == NCH - 1)
+                    def _():
+                        fetch_start(j, UNITS - 2, NKG - 2)
+                        fetch_start(j, UNITS - 1, NKG)
+
+                    arrived(s, NKG - 1)
+            with jax.named_scope('LRW'):
+                fetch_wait(NKG - 1)
+                stage_left(j, s, NKG - 1)
+                for part in range(len(NS)):
+                    stage_right(((NKG - 1, NKG - 1),), part)
+                stage_pair(j, s)
+            with jax.named_scope('after'):
+                @pl.when((j == 0) | (s < NCH - 1))
+                def _():
+                    fetch(NKG * s + 2)
             return carry
 
-        lax.fori_loop(0, 2, opening, 0)
-        first_chunk(2)
-        with jax.named_scope('L'):
-            stage_left(0, 2)
-        with jax.named_scope('r1'):
-            after(2)
-
-            @pl.when(j == 0)
-            def _():
-                r_before(3)
-            first_chunk(3)
-        with jax.named_scope('LW'):
-            stage_left(0, 3)
-            for k in range(TERMS):
-                stage_pair(k)
-        with jax.named_scope('r2'):
-            after(3)
-
-            @pl.when(j > 0)
-            def _():
-                relay_diag(4)
-                relay_xy(5)
-                send_own(7)
-
-        def chunk(c, carry):
-            def unit(g, carry):
-                q, slot = NKG * c + g, lax.rem(g, 2)
-                with jax.named_scope('before'):
-                    before(q)
-                with jax.named_scope('RL'):
-                    fetch_wait(slot)
-                    for part in range(len(NS)):
-                        stage_right(g, slot, part)
-                    stage_left(c, g)
-                with jax.named_scope('after'):
-                    after(q)
-                return carry
-
-            lax.fori_loop(0, NKG - 1, unit, 0)
-            q = NKG * c + NKG - 1
-            with jax.named_scope('before'):
-                before(q)
-            with jax.named_scope('LRW'):
-                fetch_wait(1)
-                stage_left(c, NKG - 1)
-                for part in range(len(NS)):
-                    stage_right(NKG - 1, 1, part)
-                for k in range(TERMS):
-                    stage_pair(k)
-            with jax.named_scope('after'):
-                after(q)
-            return carry
-
         lax.fori_loop(1, NCH, chunk, 0)
 
-        def tail(g, carry):
-            @pl.when(j == 0)
-            def _():
-                r_before(UNITS + g)
-            with jax.named_scope('tail'):
-                fetch_wait(lax.rem(g, 2))
-                for part in range(len(NS)):
-                    stage_right(g, lax.rem(g, 2), part)
-
-            @pl.when(g < 2)
-            def _():
-                after(UNITS + g)
-            return carry
-
-        lax.fori_loop(0, NKG - 1, tail, 0)
+        @pl.when(j == 0)
+        def _():
+            r_before(UNITS)
+            fetch(UNITS - 1, NKG)
 
         with jax.named_scope('sent'):
             @pl.when(j == 0)
@@ -454,11 +484,13 @@
                 for kind in range(NV):
                     v_sent(kind)
 
-        with jax.named_scope('last'):
-            fetch_wait(1)
+        with jax.named_scope('tail'):
+            blocks = ((0, 0), (1, 1), (2, 2), (3, NKG))
+            for _, slot in blocks:
+                fetch_wait(slot)
             b_sum, v_sum = zero, zero
             for part in range(len(NS)):
-                stage_right(NKG - 1, 1, part)
+                stage_right(blocks, part)
                 for i in range(*NS[part]):
                     at = slice(i * LANES, (i + 1) * LANES)
                     for c in range(NCH):
@@ -521,10 +553,9 @@
                     vbuf[c, p, pl.ds(pl.multiple_of(me * ROWS + 16 * a, 16), 16), :] = low[16 * t:16 * t + 16]
                 sig[cs, at] = (v * -beta).T
 
-            @pl.when((c == 1) & (j < STEPS - 1))
+            @pl.when((c < 2) & (j < STEPS - 1))
             def _():
-                send_own(0)
-                send_own(1)
+                send_own(0, c)
             return x_sum
 
         with jax.named_scope('pass3'):
@@ -553,7 +584,7 @@
             pltpu.VMEM((TERMS, ROWS, BOND), jnp.bfloat16),
             pltpu.VMEM((TERMS, 16, 16), jnp.bfloat16),
             pltpu.VMEM((TERMS, 256, 256), jnp.bfloat16),
-            pltpu.VMEM((2, BOND, KG * LANES), jnp.bfloat16),
+            pltpu.VMEM((NKG + 1, KG, BOND, LANES), jnp.bfloat16),
             pltpu.VMEM((BOND, SLAB), jnp.float32),
             pltpu.VMEM((NP, TERMS * ROWS, LANES), jnp.bfloat16),
             pltpu.VMEM((NKG, SLAB, KG * LANES), jnp.bfloat16),
@@ -561,8 +592,8 @@
             pltpu.VMEM((8, LANES), jnp.float32),
             pltpu.VMEM((8, LANES), jnp.float32),
             pltpu.VMEM((2, NDEV, 8, LANES), jnp.float32),
-            dma((NP,)), dma((SLOTS,)), dma((2,)), dma((NDEV - 1,)), dma((NDEV - 1,)), dma((NDEV - 1,)), dma((NDEV - 1,)),
-            dma((2, KG)), dma((NP,)), dma((10,)), dma((UNITS * 8,)), dma((NDEV - 1,)), dma((2, NDEV - 1)),
+            dma((NP,)), dma((SLOTS,)), dma((2,)), dma((2 * NCH,)), dma((NDEV - 1,)), dma((NDEV - 1,)), dma((NDEV - 1,)), dma((NDEV - 1,)),
+            dma((NKG + 1,)), dma((NP,)), dma((10,)), dma((UNITS * 8,)), dma((NDEV - 1,)), dma((2, NDEV - 1)),
         ],
         compiler_params=pltpu.CompilerParams(collective_id=0, has_side_effects=True, vmem_limit_bytes=67043328),
     )(psi, left, pair, right)

time: 955 us -> 925 us (0.969)
  Pallas kernels: 922 us -> 892 us
    pallas_call x1, Pallas kernels: 922 us -> 892 us  [lanczos(): pl.pallas_call(kernel, out_shape=(jax.ShapeDtypeStruct((STEPS + 1, ROWS,...]
where the time goes in v3:
time: 925 us; the launch traced here: 924 us
  Pallas kernels  892 us (96%)
  local copies, waits for them, and re-layouts  31.4 us (3%)
    pallas_call x1, Pallas kernels, lanczos(): pl.pallas_call(kernel, out_shape=(jax.ShapeDtypeStruct((STEPS + 1, ROWS,...  892 us
    unnamed x1, local copies, waits for them, and re-layouts  30 us

profile of v3, /device:TPU:0, one launch (start us, length us, event | category | flops | bytes accessed | tf_op | source)
XLA Modules:
  0.0 924.4 jit_solution(3478119469609330626)
XLA Ops:
  0.6 892.3 %shard_map.67 = (f32[7,112,4,4,896]{4,3,2,1,0:T(4,128)}, bf16[16,896,896]{2,1,0:T(8,128)(2,1)}, f32[6,8,128]{2,1,0:T(8,128)}) custom-call(f32[896,4,4,896]{3,2,1,0:T(4,128)} %psi_h.1, bf16[2,896,896]{2,1,0:T(8,128)(2,1)} %left_h.1, bf16[2,16,16]{2,1,0:T(8,128)(2,1)} %pair_h.1, bf16[2,896,896]{2,1,0:T(8,128)(2,1)} %right_h.1), custom_call_target="tpu_custom_call" | custom-call | tf_op jit(solution)/shard_map/pallas_call | solution.py:574
  892.9 1.5 slice_reduce_fusion
  894.4 30.0 %copy.8 = f32[7,112,4,4,896]{4,3,2,1,0:T(4,128)} copy(f32[7,112,4,4,896]{4,3,2,1,0:T(4,128)} %get-tuple-element.12) | data formatting | bytes 89915392

commit v4 on v3

--- a/solution.py
+++ b/solution.py
@@ -18,13 +18,14 @@
 UNITS = NCH * NKG
 SLAB = NP * ROWS
 SLOTS = SLAB // LANES
+TAIL = 96
 ELEMS = BOND * NP * BOND
 MESH = pl.DeviceIdType.MESH
 NS = ((0, 4), (4, 8), (8, 12), (12, 14))
 
 
 def kernel(psi_h, left_h, pair_h, right_h, kry_h, rall_h, ab_ref,
-           vbuf, left, wall, kron, rblk, sig, ubuf, zbuf, vec, scale, mine, exch,
+           vbuf, left, wall, kron, kmix, rblk, sig, ubuf, zbuf, vec, scale, mine, exch,
            slab_sem, psi_sem, own_sem, rest_sem, ls_sem, lr_sem, ws_sem, wr_sem,
            r_sem, out_sem, send_sem, recv_sem, xs_sem, xr_sem):
     me = lax.axis_index('terms')
@@ -49,25 +50,25 @@
     def remote(src, dst, ssem, rsem, target):
         return pltpu.make_async_remote_copy(src, dst, ssem, rsem, device_id=(target,), device_id_type=MESH)
 
-    v_kinds = ((0, 4, me, xn, xn), (0, 4, me, yn, yn), (0, 4, me, sib, sib), (0, 2, xn, yn, dg), (2, 2, yn, xn, dg),
-               (0, 4, xn, sib, sx), (0, 4, yn, sib, sy), (0, 4, dg, sib, sd))
-    NV = len(v_kinds)
+    v_kinds = ((0, 4, me, xn, 0), (0, 4, me, yn, 1), (0, 4, me, sib, 3), (0, 2, xn, yn, 2), (2, 2, yn, xn, 2),
+               (0, 4, xn, sib, 3), (0, 4, yn, sib, 3), (0, 4, dg, sib, 3))
+    v_arrivals = (4, 4, 4, 16)
+    NV = len(v_arrivals)
 
     def v_part(first, count, origin, c, g):
         return vbuf.at[c, pl.ds(4 * g + first, count), rows(origin), :]
 
-    def v_sem(c, g, kind):
-        return recv_sem.at[c * (NV * NKG) + g * NV + kind]
+    def v_sem(c, g, arrival):
+        return recv_sem.at[c * (NV * NKG) + g * NV + arrival]
 
     def v_send(c, g, kind):
-        first, count, origin, target, _ = v_kinds[kind]
+        first, count, origin, target, arrival = v_kinds[kind]
         part = v_part(first, count, origin, c, g)
-        remote(part, part, send_sem.at[kind], v_sem(c, g, kind), target).start()
-
-    def v_landed(c, g, kind):
-        first, count, _, target, origin = v_kinds[kind]
-        part = v_part(first, count, origin, c, g)
-        remote(part, part, send_sem.at[kind], v_sem(c, g, kind), target).wait_recv()
+        remote(part, part, send_sem.at[kind], v_sem(c, g, arrival), target).start()
+
+    def v_landed(c, g, arrival):
+        part = vbuf.at[c, pl.ds(0, v_arrivals[arrival]), rows(me), :]
+        remote(part, part, send_sem.at[0], v_sem(c, g, arrival), sib).wait_recv()
 
     def v_sent(kind):
         first, count, origin, target, _ = v_kinds[kind]
@@ -87,13 +88,11 @@
         v_send(c, g, 6)
 
     def relay_diag(c, g):
+        v_landed(c, g, 2)
+        v_send(c, g, 7)
+
+    def arrived(c, g):
         v_landed(c, g, 3)
-        v_landed(c, g, 4)
-        v_send(c, g, 7)
-
-    def arrived(c, g):
-        for kind in (2, 5, 6, 7):
-            v_landed(c, g, kind)
 
     LO, HI, ALL = (0, 1), (1, 1), (0, 2)
     r_kinds = ((LO, me, xn, xn), (HI, me, xn, xn), (HI, me, yn, yn), (LO, me, yn, yn), (ALL, me, sib, sib),
@@ -122,9 +121,15 @@
     def left_copy(n):
         return remote(left_h.at[:, rows(others[n]), :], left.at[pl.ds(2 * me, 2)], ls_sem.at[n], lr_sem.at[n], others[n])
 
+    def regroup(dev):
+        a, b = (left[2 * dev + h, TAIL:ROWS, :].astype(jnp.float32) for h in range(2))
+        left[2 * dev, TAIL:ROWS, :] = jnp.concatenate([a[:8], b[:8]], axis=0).astype(jnp.bfloat16)
+        left[2 * dev + 1, TAIL:ROWS, :] = jnp.concatenate([a[8:], b[8:]], axis=0).astype(jnp.bfloat16)
+
     def left_landed(n):
         part = left.at[pl.ds(2 * others[n], 2)]
         remote(part, part, ls_sem.at[n], lr_sem.at[n], others[n]).wait_recv()
+        regroup(others[n])
 
     def pair_copy(n):
         return remote(pair_h, wall.at[pl.ds(2 * me, 2)], ws_sem.at[n], wr_sem.at[n], others[n])
@@ -178,6 +183,10 @@
     for n in range(SLOTS):
         psi_copy(n).start()
     zero = jnp.zeros((8, LANES), jnp.float32)
+    with jax.named_scope('barrier'):
+        pl.semaphore_wait(barrier, NDEV - 1)
+    for n in (0, 1, 3):
+        left_copy(n).start()
     for cp in slab:
         cp.wait()
 
@@ -189,12 +198,10 @@
         return acc
 
     mine[...] = jnp.full((8, LANES), jnp.sum(lax.fori_loop(0, SLOTS, squares, zero, unroll=2)))
-    with jax.named_scope('barrier'):
-        pl.semaphore_wait(barrier, NDEV - 1)
     copies = exchange_start(1)
     for n in range(NDEV - 1):
         pair_copy(n).start()
-    for n in range(5):
+    for n in (2, 4):
         left_copy(n).start()
 
     def r_own(c):
@@ -258,6 +265,15 @@
     with jax.named_scope('convert'):
         lax.fori_loop(0, TERMS, opening_pieces, 0)
     left_landed(0)
+    regroup(me)
+    first_half = lax.rem(lax.broadcasted_iota(jnp.int32, (256, 256), 0), 16) < 8
+
+    def mix(n, carry):
+        kmix[n] = jnp.where(first_half, kron[2 * n].astype(jnp.float32),
+                            kron[2 * n + 1].astype(jnp.float32)).astype(jnp.bfloat16)
+        return carry
+
+    lax.fori_loop(0, TERMS // 2, mix, 0)
     with jax.named_scope('ownwait'):
         for cp in place_own:
             cp.wait()
@@ -296,15 +312,28 @@
     def stage_pair(j, s):
         for i in range(NKG):
             _, _, kg = place(j, NKG * s + i)
+
+            def columns(row):
+                return ubuf[:, row:row + 16, :].reshape(256, LANES)
+
             for k in range(KG):
                 row, at = (i * KG + k) * ROWS, k * LANES
-                rhs = jnp.concatenate([ubuf[:, row + g * 16:row + (g + 1) * 16, :].reshape(256, LANES)
-                                       for g in range(ROWS // 16)], axis=1)
+                rhs = jnp.concatenate([columns(row + g * 16) for g in range(TAIL // 16)], axis=1)
                 o = jnp.dot(kron[kg * KG + k], rhs, preferred_element_type=jnp.float32).astype(jnp.bfloat16)
-                for g in range(ROWS // 16):
+                for g in range(TAIL // 16):
                     for q in range(NP):
                         zbuf[i, q * ROWS + g * 16:q * ROWS + (g + 1) * 16, at:at + LANES] = (
                             o[q * 16:(q + 1) * 16, g * LANES:(g + 1) * LANES])
+            for n in range(KG // 2):
+                row = (i * KG + 2 * n) * ROWS + TAIL
+                rhs = jnp.concatenate([columns(row), columns(row + ROWS)], axis=1)
+                o = jnp.dot(kmix[kg * (KG // 2) + n], rhs, preferred_element_type=jnp.float32)
+                for h in range(2):
+                    at = (2 * n + h) * LANES
+                    for q in range(NP):
+                        half = o[q * 16 + 8 * h:q * 16 + 8 * h + 8]
+                        zbuf[i, q * ROWS + TAIL:(q + 1) * ROWS, at:at + LANES] = jnp.concatenate(
+                            [half[:, :LANES], half[:, LANES:]], axis=0).astype(jnp.bfloat16)
 
     def stage_right(blocks, part):
         n0, n1 = NS[part][0] * LANES, NS[part][1] * LANES
@@ -481,7 +510,7 @@
 
             @pl.when(j > 0)
             def _():
-                for kind in range(NV):
+                for kind in range(len(v_kinds)):
                     v_sent(kind)
 
         with jax.named_scope('tail'):
@@ -584,6 +613,7 @@
             pltpu.VMEM((TERMS, ROWS, BOND), jnp.bfloat16),
             pltpu.VMEM((TERMS, 16, 16), jnp.bfloat16),
             pltpu.VMEM((TERMS, 256, 256), jnp.bfloat16),
+            pltpu.VMEM((TERMS // 2, 256, 256), jnp.bfloat16),
             pltpu.VMEM((NKG + 1, KG, BOND, LANES), jnp.bfloat16),
             pltpu.VMEM((BOND, SLAB), jnp.float32),
             pltpu.VMEM((NP, TERMS * ROWS, LANES), jnp.bfloat16),
@@ -593,7 +623,7 @@
             pltpu.VMEM((8, LANES), jnp.float32),
             pltpu.VMEM((2, NDEV, 8, LANES), jnp.float32),
             dma((NP,)), dma((SLOTS,)), dma((2,)), dma((2 * NCH,)), dma((NDEV - 1,)), dma((NDEV - 1,)), dma((NDEV - 1,)), dma((NDEV - 1,)),
-            dma((NKG + 1,)), dma((NP,)), dma((10,)), dma((UNITS * 8,)), dma((NDEV - 1,)), dma((2, NDEV - 1)),
+            dma((NKG + 1,)), dma((NP,)), dma((10,)), dma((UNITS * 4,)), dma((NDEV - 1,)), dma((2, NDEV - 1)),
         ],
         compiler_params=pltpu.CompilerParams(collective_id=0, has_side_effects=True, vmem_limit_bytes=67043328),
     )(psi, left, pair, right)

time: 925 us -> 914 us (0.988)
  Pallas kernels: 892 us -> 881 us
    pallas_call x1, Pallas kernels: 892 us -> 881 us  [lanczos(): pl.pallas_call(kernel, out_shape=(jax.ShapeDtypeStruct((STEPS + 1, ROWS,...]
where the time goes in v4:
time: 914 us; the launch traced here: 913 us
  Pallas kernels  881 us (96%)
  local copies, waits for them, and re-layouts  31.4 us (3%)
    pallas_call x1, Pallas kernels, lanczos(): pl.pallas_call(kernel, out_shape=(jax.ShapeDtypeStruct((STEPS + 1, ROWS,...  881 us
    unnamed x1, local copies, waits for them, and re-layouts  30 us

profile of v4, /device:TPU:0, one launch (start us, length us, event | category | flops | bytes accessed | tf_op | source)
XLA Modules:
  0.0 913.5 jit_solution(1405758993353660369)
XLA Ops:
  0.6 881.4 %shard_map.67 = (f32[7,112,4,4,896]{4,3,2,1,0:T(4,128)}, bf16[16,896,896]{2,1,0:T(8,128)(2,1)}, f32[6,8,128]{2,1,0:T(8,128)}) custom-call(f32[896,4,4,896]{3,2,1,0:T(4,128)} %psi_h.1, bf16[2,896,896]{2,1,0:T(8,128)(2,1)} %left_h.1, bf16[2,16,16]{2,1,0:T(8,128)(2,1)} %pair_h.1, bf16[2,896,896]{2,1,0:T(8,128)(2,1)} %right_h.1), custom_call_target="tpu_custom_call" | custom-call | tf_op jit(solution)/shard_map/pallas_call | solution.py:603
  882.0 1.5 slice_reduce_fusion
  883.5 30.0 %copy.8 = f32[7,112,4,4,896]{4,3,2,1,0:T(4,128)} copy(f32[7,112,4,4,896]{4,3,2,1,0:T(4,128)} %get-tuple-element.12) | data formatting | bytes 89915392

commit v5 on v4

--- a/solution.py
+++ b/solution.py
@@ -118,8 +118,9 @@
         part = rall_h.at[pl.ds(2 * origin + half[0], half[1])]
         remote(part, part, send_sem.at[kind], recv_sem.at[kind], target).wait_send()
 
-    def left_copy(n):
-        return remote(left_h.at[:, rows(others[n]), :], left.at[pl.ds(2 * me, 2)], ls_sem.at[n], lr_sem.at[n], others[n])
+    def left_copy(n, h):
+        return remote(left_h.at[h, rows(others[n]), :], left.at[2 * me + h], ls_sem.at[2 * n + h], lr_sem.at[2 * n + h],
+                      others[n])
 
     def regroup(dev):
         a, b = (left[2 * dev + h, TAIL:ROWS, :].astype(jnp.float32) for h in range(2))
@@ -127,8 +128,9 @@
         left[2 * dev + 1, TAIL:ROWS, :] = jnp.concatenate([a[8:], b[8:]], axis=0).astype(jnp.bfloat16)
 
     def left_landed(n):
-        part = left.at[pl.ds(2 * others[n], 2)]
-        remote(part, part, ls_sem.at[n], lr_sem.at[n], others[n]).wait_recv()
+        for h in range(2):
+            part = left.at[2 * others[n] + h]
+            remote(part, part, ls_sem.at[2 * n + h], lr_sem.at[2 * n + h], others[n]).wait_recv()
         regroup(others[n])
 
     def pair_copy(n):
@@ -146,6 +148,11 @@
     def vector_out(j):
         return [pltpu.make_async_copy(vec.at[pl.ds(p * ROWS, ROWS), :], kry_h.at[j, :, p // 4, p % 4, :],
                                       out_sem.at[p]) for p in range(NP)]
+
+    def chunk_out(j, c):
+        for p in range(NP):
+            pltpu.make_async_copy(vec.at[pl.ds(p * ROWS, ROWS), lanes(c)], kry_h.at[j, :, p // 4, p % 4, lanes(c)],
+                                  out_sem.at[p]).start()
 
     def fold(x):
         return jnp.sum(x.reshape(-1, 8, LANES), axis=0)
@@ -185,8 +192,8 @@
     zero = jnp.zeros((8, LANES), jnp.float32)
     with jax.named_scope('barrier'):
         pl.semaphore_wait(barrier, NDEV - 1)
-    for n in (0, 1, 3):
-        left_copy(n).start()
+    for n, h in ((1, 0), (3, 0), (0, 0), (0, 1)):
+        left_copy(n, h).start()
     for cp in slab:
         cp.wait()
 
@@ -201,8 +208,8 @@
     copies = exchange_start(1)
     for n in range(NDEV - 1):
         pair_copy(n).start()
-    for n in (2, 4):
-        left_copy(n).start()
+    for n, h in ((1, 1), (3, 1), (2, 0), (4, 0), (2, 1), (4, 1)):
+        left_copy(n, h).start()
 
     def r_own(c):
         for kind in (4, 0, 2, 1, 3):
@@ -214,7 +221,8 @@
 
     lax.fori_loop(0, 5, operators_out, 0)
     for n in (5, 6):
-        left_copy(n).start()
+        for h in range(2):
+            left_copy(n, h).start()
     lax.fori_loop(5, NCH, operators_out, 0)
     for cp in take:
         cp.wait()
@@ -505,7 +513,8 @@
                 for kind in range(NR):
                     r_sent(kind)
                 for n in range(NDEV - 1):
-                    left_copy(n).wait_send()
+                    for h in range(2):
+                        left_copy(n, h).wait_send()
                     pair_copy(n).wait_send()
 
             @pl.when(j > 0)
@@ -585,12 +594,12 @@
             @pl.when((c < 2) & (j < STEPS - 1))
             def _():
                 send_own(0, c)
+
+            chunk_out(j + 1, c)
             return x_sum
 
         with jax.named_scope('pass3'):
             x_sum = lax.fori_loop(0, NCH, third, zero)
-        for cp in vector_out(j + 1):
-            cp.start()
         return beta, jnp.full((8, LANES), jnp.sum(x_sum))
 
     lax.fori_loop(0, STEPS, one_step, (jnp.zeros((1, LANES), jnp.float32), zero))
@@ -622,7 +631,7 @@
             pltpu.VMEM((8, LANES), jnp.float32),
             pltpu.VMEM((8, LANES), jnp.float32),
             pltpu.VMEM((2, NDEV, 8, LANES), jnp.float32),
-            dma((NP,)), dma((SLOTS,)), dma((2,)), dma((2 * NCH,)), dma((NDEV - 1,)), dma((NDEV - 1,)), dma((NDEV - 1,)), dma((NDEV - 1,)),
+            dma((NP,)), dma((SLOTS,)), dma((2,)), dma((2 * NCH,)), dma((14,)), dma((14,)), dma((NDEV - 1,)), dma((NDEV - 1,)),
             dma((NKG + 1,)), dma((NP,)), dma((10,)), dma((UNITS * 4,)), dma((NDEV - 1,)), dma((2, NDEV - 1)),
         ],
         compiler_params=pltpu.CompilerParams(collective_id=0, has_side_effects=True, vmem_limit_bytes=67043328),

time: 914 us -> 912 us (level)
  no operation moved by 1% of the time
where the time goes in v5:
time: 912 us; the launch traced here: 911 us
  Pallas kernels  879 us (96%)
  local copies, waits for them, and re-layouts  31.4 us (3%)
    pallas_call x1, Pallas kernels, lanczos(): pl.pallas_call(kernel, out_shape=(jax.ShapeDtypeStruct((STEPS + 1, ROWS,...  879 us
    unnamed x1, local copies, waits for them, and re-layouts  30 us

profile of v5, /device:TPU:0, one launch (start us, length us, event | category | flops | bytes accessed | tf_op | source)
XLA Modules:
  0.0 911.3 jit_solution(2789100460133714985)
XLA Ops:
  0.6 879.3 %shard_map.67 = (f32[7,112,4,4,896]{4,3,2,1,0:T(4,128)}, bf16[16,896,896]{2,1,0:T(8,128)(2,1)}, f32[6,8,128]{2,1,0:T(8,128)}) custom-call(f32[896,4,4,896]{3,2,1,0:T(4,128)} %psi_h.1, bf16[2,896,896]{2,1,0:T(8,128)(2,1)} %left_h.1, bf16[2,16,16]{2,1,0:T(8,128)(2,1)} %pair_h.1, bf16[2,896,896]{2,1,0:T(8,128)(2,1)} %right_h.1), custom_call_target="tpu_custom_call" | custom-call | tf_op jit(solution)/shard_map/pallas_call | solution.py:612
  879.9 1.5 slice_reduce_fusion
  881.4 30.0 %copy.8 = f32[7,112,4,4,896]{4,3,2,1,0:T(4,128)} copy(f32[7,112,4,4,896]{4,3,2,1,0:T(4,128)} %get-tuple-element.12) | data formatting | bytes 89915392

commit v6 on v5

--- a/solution.py
+++ b/solution.py
@@ -447,8 +447,6 @@
 
                     @pl.when(j > 0)
                     def _():
-                        relay_diag(s, g + 1)
-
                         @pl.when(NKG * s + g < UNITS - 2)
                         def _():
                             ahead = g + 2
@@ -458,6 +456,7 @@
                         def _():
                             send_own(s + 1, g)
 
+                        relay_diag(s, g + 1)
                         arrived(s, g)
                 with jax.named_scope('RL'):
                     fetch_wait(g)
@@ -542,7 +541,8 @@
         b_row = jnp.full((8, LANES), jnp.sum(b_sum))
         v_row = jnp.full((8, LANES), jnp.sum(v_sum))
         a_row = b_row + beta_prev * cross
-        fit = jnp.where(v_row > 0, b_row / jnp.where(v_row > 0, v_row, 1.0), 0.0)
+        held = v_row > 1e-20
+        fit = jnp.where(held, b_row / jnp.where(held, v_row, 1.0), 0.0)
         fit_row = fit[0:1, :]
 
         def second(i, n_sum):
@@ -560,7 +560,7 @@
 
         row_id = lax.broadcasted_iota(jnp.int32, (8, LANES), 0)
         mine[...] = jnp.where(row_id == 0, a_row, jnp.where(
-            row_id == 1, v_row, jnp.where(row_id == 2, fit, jnp.full((8, LANES), n_loc))))
+            row_id == 1, jnp.sqrt(v_row), jnp.where(row_id == 2, fit, jnp.full((8, LANES), n_loc))))
         par = lax.rem(j, 2)
         with jax.named_scope('exch'):
             exchange_wait(par, exchange_start(par))
@@ -571,8 +571,8 @@
         square = jnp.zeros((1, LANES), jnp.float32)
         for d in range(NDEV):
             part = exch[par, d]
-            gap = alpha - part[2:3, :]
-            square = square + (part[3:4, :] + gap * gap * part[1:2, :])
+            gap = (alpha - part[2:3, :]) * part[1:2, :]
+            square = square + (part[3:4, :] + gap * gap)
         beta = jnp.sqrt(square * (1.0 / ELEMS))
         inv = 1.0 / beta
         ab_ref[j] = jnp.concatenate([alpha, beta] + [alpha] * 6, axis=0)

time: 912 us -> 912 us (level)
  no operation moved by 1% of the time
where the time goes in v6:
time: 912 us; the launch traced here: 911 us
  Pallas kernels  879 us (96%)
  local copies, waits for them, and re-layouts  31.4 us (3%)
    pallas_call x1, Pallas kernels, lanczos(): pl.pallas_call(kernel, out_shape=(jax.ShapeDtypeStruct((STEPS + 1, ROWS,...  879 us
    unnamed x1, local copies, waits for them, and re-layouts  30 us

profile of v6, /device:TPU:0, one launch (start us, length us, event | category | flops | bytes accessed | tf_op | source)
XLA Modules:
  0.0 911.4 jit_solution(8418985827958825633)
XLA Ops:
  0.6 879.3 %shard_map.67 = (f32[7,112,4,4,896]{4,3,2,1,0:T(4,128)}, bf16[16,896,896]{2,1,0:T(8,128)(2,1)}, f32[6,8,128]{2,1,0:T(8,128)}) custom-call(f32[896,4,4,896]{3,2,1,0:T(4,128)} %psi_h.1, bf16[2,896,896]{2,1,0:T(8,128)(2,1)} %left_h.1, bf16[2,16,16]{2,1,0:T(8,128)(2,1)} %pair_h.1, bf16[2,896,896]{2,1,0:T(8,128)(2,1)} %right_h.1), custom_call_target="tpu_custom_call" | custom-call | tf_op jit(solution)/shard_map/pallas_call | solution.py:612
  879.9 1.5 slice_reduce_fusion
  881.4 30.0 %copy.8 = f32[7,112,4,4,896]{4,3,2,1,0:T(4,128)} copy(f32[7,112,4,4,896]{4,3,2,1,0:T(4,128)} %get-tuple-element.12) | data formatting | bytes 89915392

commit v7 on v6

--- a/solution.py
+++ b/solution.py
@@ -157,6 +157,9 @@
     def fold(x):
         return jnp.sum(x.reshape(-1, 8, LANES), axis=0)
 
+    def everywhere(x):
+        return jnp.broadcast_to(jnp.sum(jnp.sum(x, axis=0, keepdims=True), axis=1, keepdims=True), (8, LANES))
+
     def exchange_start(par):
         exch[par, me] = mine[...]
         copies = [remote(mine, exch.at[par, me], xs_sem.at[n], xr_sem.at[par, n], others[n]) for n in range(NDEV - 1)]
@@ -167,9 +170,6 @@
     def exchange_wait(par, copies):
         for n in range(NDEV - 1):
             remote(mine, exch.at[par, others[n]], xs_sem.at[n], xr_sem.at[par, n], others[n]).wait_recv()
-        for cp in copies:
-            cp.wait_send()
-
     barrier = pltpu.get_barrier_semaphore()
     for n in range(NDEV - 1):
         pl.semaphore_signal(barrier, inc=1, device_id=(others[n],), device_id_type=MESH)
@@ -230,6 +230,8 @@
         cp.start()
     with jax.named_scope('exch0'):
         exchange_wait(1, copies)
+        for cp in copies:
+            cp.wait_send()
     total = exch[1, 0]
     for d in range(1, NDEV):
         total = total + exch[1, d]
@@ -538,8 +540,7 @@
                         b_sum = b_sum + fold(s * v)
                         v_sum = v_sum + fold(v * v)
 
-        b_row = jnp.full((8, LANES), jnp.sum(b_sum))
-        v_row = jnp.full((8, LANES), jnp.sum(v_sum))
+        b_row, v_row = everywhere(b_sum), everywhere(v_sum)
         a_row = b_row + beta_prev * cross
         held = v_row > 1e-20
         fit = jnp.where(held, b_row / jnp.where(held, v_row, 1.0), 0.0)
@@ -554,16 +555,17 @@
             return n_sum
 
         with jax.named_scope('pass2'):
-            n_loc = jnp.sum(lax.fori_loop(0, SLOTS, second, zero, unroll=2))
+            n_row = everywhere(lax.fori_loop(0, SLOTS, second, zero, unroll=2))
         for cp in vector_out(j):
             cp.wait()
 
         row_id = lax.broadcasted_iota(jnp.int32, (8, LANES), 0)
         mine[...] = jnp.where(row_id == 0, a_row, jnp.where(
-            row_id == 1, jnp.sqrt(v_row), jnp.where(row_id == 2, fit, jnp.full((8, LANES), n_loc))))
+            row_id == 1, jnp.sqrt(v_row), jnp.where(row_id == 2, fit, n_row)))
         par = lax.rem(j, 2)
         with jax.named_scope('exch'):
-            exchange_wait(par, exchange_start(par))
+            copies = exchange_start(par)
+            exchange_wait(par, copies)
         total = exch[par, 0]
         for d in range(1, NDEV):
             total = total + exch[par, d]
@@ -600,7 +602,9 @@
 
         with jax.named_scope('pass3'):
             x_sum = lax.fori_loop(0, NCH, third, zero)
-        return beta, jnp.full((8, LANES), jnp.sum(x_sum))
+        for cp in copies:
+            cp.wait_send()
+        return beta, everywhere(x_sum)
 
     lax.fori_loop(0, STEPS, one_step, (jnp.zeros((1, LANES), jnp.float32), zero))
     for cp in vector_out(STEPS):

time: 912 us -> 911 us (level)
  no operation moved by 1% of the time
where the time goes in v7:
time: 911 us
  Pallas kernels  879 us (96%)
  local copies, waits for them, and re-layouts  31.4 us (3%)
    pallas_call x1, Pallas kernels, lanczos(): pl.pallas_call(kernel, out_shape=(jax.ShapeDtypeStruct((STEPS + 1, ROWS,...  879 us
    unnamed x1, local copies, waits for them, and re-layouts  30 us

profile of v7, /device:TPU:0, one launch (start us, length us, event | category | flops | bytes accessed | tf_op | source)
XLA Modules:
  0.0 910.9 jit_solution(11536166064590609143)
XLA Ops:
  0.6 878.8 %shard_map.67 = (f32[7,112,4,4,896]{4,3,2,1,0:T(4,128)}, bf16[16,896,896]{2,1,0:T(8,128)(2,1)}, f32[6,8,128]{2,1,0:T(8,128)}) custom-call(f32[896,4,4,896]{3,2,1,0:T(4,128)} %psi_h.1, bf16[2,896,896]{2,1,0:T(8,128)(2,1)} %left_h.1, bf16[2,16,16]{2,1,0:T(8,128)(2,1)} %pair_h.1, bf16[2,896,896]{2,1,0:T(8,128)(2,1)} %right_h.1), custom_call_target="tpu_custom_call" | custom-call | tf_op jit(solution)/shard_map/pallas_call | solution.py:616
  879.4 1.5 slice_reduce_fusion
  880.9 30.0 %copy.8 = f32[7,112,4,4,896]{4,3,2,1,0:T(4,128)} copy(f32[7,112,4,4,896]{4,3,2,1,0:T(4,128)} %get-tuple-element.12) | data formatting | bytes 89915392
